TPU v7x, 32 devices: a whole 2x2x4 slice. The times are simulated.
32 devices in a mesh: seq: 4 (over x, core), tensor: 8 (over z, y).
Axes of the slice: x: 2, y: 2, z: 4, core: 2. Of those that a mesh axis runs over, the one named last changes fastest.
Arguments:
- tokens: bfloat16 [2, 4096, 4096], P(None, 'seq', 'tensor'), may hold values from -6 to 6
- w_qkv: bfloat16 [4096, 3, 4096], P(None, None, 'tensor'), may hold values from -1 to 1
- q_gain: float32 [4096], P('tensor'), may hold values from 0.5 to 2.5
- k_gain: float32 [4096], P('tensor'), may hold values from 0.5 to 2.5
- w_out: bfloat16 [4096, 4096], P('tensor'), may hold values from -0.125 to 0.125
Outputs:
- mixed: bfloat16 [2, 4096, 4096], P(None, 'seq', 'tensor')
- peak: float32 [32], P('tensor')
- qk_scale: float32 [2, 2, 4096], P(None, None, 'seq')
All inputs are finite; a program needn't handle non-finite values.
Results may differ from a plain program's by a relative error of at most 0.024.
Values may be sent and summed in bfloat16 or wider, within the bound.
A program may use at most 128 MiB of HBM per device.

v0:
```python
import functools

import jax
import jax.numpy as jnp
from jax import lax
from jax.experimental import pallas as pl
from jax.experimental.pallas import tpu as pltpu
from jax.sharding import PartitionSpec as P


HEADS = 32
EPS = 1e-06
ROPE_BASE = 500000.0
NEG = -1e30
LOG2E = 1.4426950408889634
BLOCK_Q = 512
BLOCK_K = 1024


def rope_tables(positions, head):
    half = head // 2
    freq = ROPE_BASE ** (-(jnp.arange(half, dtype=jnp.float32) * 2.0) / head)
    angle = positions[:, None] * freq[None, :]
    cosine, sine = jnp.cos(angle), jnp.sin(angle)
    return (
        jnp.concatenate([cosine, cosine], -1),
        jnp.concatenate([-sine, sine], -1),
    )


def flash_kernel(use_ref, q_ref, *refs, blocks, bq, bk):
    k_refs, v_refs = refs[:blocks], refs[blocks : 2 * blocks]
    o_ref, top_ref, m_s, l_s, acc_s = refs[2 * blocks :]
    rows = q_ref.shape[0]
    best = jnp.full((1, 128), NEG, jnp.float32)
    for i in range(rows // bq):
        q = q_ref[pl.ds(i * bq, bq), :]
        m_s[...] = jnp.full(m_s.shape, NEG, jnp.float32)
        l_s[...] = jnp.zeros(l_s.shape, jnp.float32)
        acc_s[...] = jnp.zeros(acc_s.shape, jnp.float32)

        def step(k, v, masked):
            s = lax.dot_general(q, k, (((1,), (1,)), ((), ())), preferred_element_type=jnp.float32)
            if masked:
                row = lax.broadcasted_iota(jnp.int32, s.shape, 0)
                col = lax.broadcasted_iota(jnp.int32, s.shape, 1)
                s = jnp.where(col <= row, s, NEG)
            m_old = m_s[...]
            m_new = jnp.maximum(m_old, jnp.max(s, -1, keepdims=True))
            p = jnp.exp2(s - jnp.tile(m_new, (1, s.shape[1] // 128)))
            alpha = jnp.exp2(m_old - m_new)
            part = p[:, :128]
            for j in range(1, s.shape[1] // 128):
                part = part + p[:, j * 128 : (j + 1) * 128]
            l_s[...] = l_s[...] * alpha + part
            acc_s[...] = acc_s[...] * alpha + jnp.dot(
                p.astype(jnp.bfloat16), v, preferred_element_type=jnp.float32
            )
            m_s[...] = m_new

        step(k_refs[0][pl.ds(i * bq, bq), :], v_refs[0][pl.ds(i * bq, bq), :], True)
        for j in range(i):
            step(k_refs[0][pl.ds(j * bq, bq), :], v_refs[0][pl.ds(j * bq, bq), :], False)
        for e in range(1, blocks):

            @pl.when(use_ref[e] > 0)
            def _():
                for j in range(rows // bk):
                    step(k_refs[e][pl.ds(j * bk, bk), :], v_refs[e][pl.ds(j * bk, bk), :], False)

        denom = jnp.sum(l_s[...], -1, keepdims=True)
        o_ref[pl.ds(i * bq, bq), :] = (acc_s[...] / denom).astype(o_ref.dtype)
        best = jnp.maximum(best, jnp.max(m_s[...], 0, keepdims=True))
    top_ref[...] = jnp.broadcast_to(best, top_ref.shape)


def flash(q, keys, values, use, head):
    rows, dloc = q.shape
    heads = dloc // head
    blocks = len(keys)
    bq = min(BLOCK_Q, rows)
    bk = min(BLOCK_K, rows)
    spec = pl.BlockSpec((rows, head), lambda h, f: (0, h))
    return pl.pallas_call(
        functools.partial(flash_kernel, blocks=blocks, bq=bq, bk=bk),
        grid_spec=pltpu.PrefetchScalarGridSpec(
            num_scalar_prefetch=1,
            grid=(heads,),
            in_specs=[spec] * (1 + 2 * blocks),
            out_specs=[spec, pl.BlockSpec((None, 8, 128), lambda h, f: (h, 0, 0))],
            scratch_shapes=[
                pltpu.VMEM((bq, 128), jnp.float32),
                pltpu.VMEM((bq, 128), jnp.float32),
                pltpu.VMEM((bq, head), jnp.float32),
            ],
        ),
        out_shape=[
            jax.ShapeDtypeStruct((rows, dloc), jnp.bfloat16),
            jax.ShapeDtypeStruct((heads, 8, 128), jnp.float32),
        ],
        compiler_params=pltpu.CompilerParams(
            dimension_semantics=("arbitrary",), vmem_limit_bytes=32 * 1024 * 1024
        ),
        cost_estimate=pl.CostEstimate(
            flops=8 * rows * rows * blocks * dloc,
            bytes_accessed=4 * rows * blocks * dloc,
            transcendentals=0,
        ),
    )(use, q, *keys, *values)


def swapped(value, axis, bit):
    size = lax.axis_size(axis)
    return lax.ppermute(value, axis, [(i, i ^ bit) for i in range(size)])


def earlier_blocks(block, count, across):
    outer = [
        lax.ppermute(block, "seq", [(i, i + across * d) for i in range(count - across * d)])
        for d in range(1, count // across)
    ]
    near = swapped(block, "seq", 1)
    return [block, near] + outer + [swapped(got, "seq", 1) for got in outer]


MESH = pl.DeviceIdType.MESH


def gather_kernel(
    tok_ref, o_ref, next_ref, up_ref, dn_ref, hold, local, up_s, up_r, dn_s, dn_r, y_s, y_r, e_s, e_r, *, line
):
    x_ref = tok_ref.at[0]
    me = lax.axis_index("tensor")
    at = me // 2
    top = line - 1
    above, below = me + 2, me - 2
    peer = me + 1 - 2 * lax.rem(me, 2)
    size = 2 * line

    barrier = pltpu.get_barrier_semaphore()
    for other in (lax.rem(me + 2, size), lax.rem(me + size - 2, size), peer):
        pl.semaphore_signal(barrier, inc=1, device_id={"tensor": other}, device_id_type=MESH)
    pl.semaphore_wait(barrier, 3)

    def send(src, dst, send_sem, recv_sem, device):
        return pltpu.make_async_remote_copy(
            src_ref=src,
            dst_ref=dst,
            send_sem=send_sem,
            recv_sem=recv_sem,
            device_id={"tensor": device},
            device_id_type=MESH,
        )

    def slot(index):
        return o_ref.at[jnp.clip(index, 0, size - 1)]

    def up(k):
        src = x_ref if k == 1 else slot(me - 2 * (k - 1))
        return send(src, slot(me - 2 * (k - 1)), up_s.at[k], up_r.at[k], jnp.minimum(above, size - 1))

    def down(k):
        src = x_ref if k == 1 else slot(me + 2 * (k - 1))
        return send(src, slot(me + 2 * (k - 1)), dn_s.at[k], dn_r.at[k], jnp.maximum(below, 0))

    def across(k):
        index = me + 2 * k
        src = x_ref if k == 0 else slot(index)
        return send(src, slot(index), y_s.at[k + top], y_r.at[k + top], peer)

    def next_up():
        return send(tok_ref.at[1], up_ref, e_s.at[0], e_r.at[0], jnp.minimum(above, size - 1))

    def next_down():
        return send(tok_ref.at[1], dn_ref, e_s.at[1], e_r.at[1], jnp.maximum(below, 0))

    @pl.when(at < top)
    def _():
        up(1).start()

    @pl.when(at > 0)
    def _():
        down(1).start()

    across(0).start()
    ins = [pltpu.make_async_copy(tok_ref.at[i], hold.at[i], local.at[i]) for i in range(2)]
    outs = [
        pltpu.make_async_copy(hold.at[0], o_ref.at[me], local.at[2]),
        pltpu.make_async_copy(hold.at[1], next_ref, local.at[3]),
    ]
    for copy in ins:
        copy.start()
    for copy, out in zip(ins, outs):
        copy.wait()
        out.start()
    for k in range(1, line):

        @pl.when(at >= k)
        def _():
            up(k).wait_recv()
            if k + 1 < line:

                @pl.when(at < top)
                def _():
                    up(k + 1).start()

            across(-k).start()

        @pl.when(at + k <= top)
        def _():
            down(k).wait_recv()
            if k + 1 < line:

                @pl.when(at > 0)
                def _():
                    down(k + 1).start()

            across(k).start()

    @pl.when(at < top)
    def _():
        next_up().start()

    @pl.when(at > 0)
    def _():
        next_down().start()

    for out in outs:
        out.wait()
    for k in range(1, line):

        @pl.when((at >= k - 1) & (at < top))
        def _():
            up(k).wait_send()

        @pl.when((at + k - 1 <= top) & (at > 0))
        def _():
            down(k).wait_send()

    for k in range(-top, line):

        @pl.when((at + k >= 0) & (at + k <= top))
        def _():
            across(k).wait()

    @pl.when(at < top)
    def _():
        next_up().wait_send()
        next_down().wait_recv()

    @pl.when(at > 0)
    def _():
        next_down().wait_send()
        next_up().wait_recv()


def gather_first(tokens, n):
    line = n // 2
    rows, depth = tokens.shape[1:]
    dma = pltpu.SemaphoreType.DMA
    piece = jax.ShapeDtypeStruct((rows, depth), tokens.dtype)
    return pl.pallas_call(
        functools.partial(gather_kernel, line=line),
        in_specs=[pl.BlockSpec(memory_space=pl.ANY)],
        out_specs=[pl.BlockSpec(memory_space=pl.ANY)] * 4,
        out_shape=[jax.ShapeDtypeStruct((n, rows, depth), tokens.dtype)] + [piece] * 3,
        scratch_shapes=[pltpu.VMEM((2, rows, depth), tokens.dtype), dma((4,))]
        + [dma((line,))] * 4
        + [dma((n,))] * 2
        + [dma((2,))] * 2,
        compiler_params=pltpu.CompilerParams(collective_id=0, has_side_effects=True),
        cost_estimate=pl.CostEstimate(
            flops=90000000000, bytes_accessed=2 * n * rows * depth, transcendentals=0
        ),
    )(tokens)


def gather_rest(own, up, down, n):
    line = n // 2
    top = line - 1

    def moved(value, pairs):
        return lax.ppermute(value, "tensor", pairs)

    def across(value, keep):
        return moved(value, [(t, t ^ 1) for t in range(n) if keep(t // 2)])

    def sides(up, down, k):
        return [
            (up, -k, 0),
            (down, k, 0),
            (across(up, lambda u: u >= k), -k, 1),
            (across(down, lambda u: u + k <= top), k, 1),
        ]

    def farther(up, down, k):
        return (
            moved(up, [(t, t + 2) for t in range(n) if k - 1 <= t // 2 < top]),
            moved(down, [(t, t - 2) for t in range(n) if 0 < t // 2 <= line - k]),
        )

    pieces = [(own, 0, 0), (moved(own, [(t, t ^ 1) for t in range(n)]), 0, 1)]
    near = up, down
    for k in range(1, line):
        ahead = farther(up, down, k + 1) if k + 1 < line else None
        if k == 1:
            near = yield near
            pieces += sides(*near, 1)
            ahead = (yield ahead) if ahead else None
        else:
            pieces += sides(up, down, k)
        if ahead:
            up, down = ahead
    yield pieces


def project_kernel(*refs, plan, parts, head, plain):
    count = max(1, len(plan))
    sources = refs[:count]
    w_ref, gain_ref, cos_ref, sin_ref = refs[count : count + 4]
    outs = 3 if plain else 2
    out, sum_ref = refs[count + 4 : count + 6]
    v_ref = refs[count + 6] if plain else None
    held, kept, lanes, mine, got, column, sems, send, recv = refs[count + 4 + outs :]
    n, rows, depth = held.shape
    tile = kept.shape[2]
    j = pl.program_id(0)
    me = lax.axis_index("tensor")
    peers = [lax.rem(me + d, n) for d in range(1, n)]

    last = (2 if plain else 1) * parts - 1
    copies = [
        pltpu.make_async_remote_copy(
            src_ref=mine,
            dst_ref=got.at[d],
            send_sem=send.at[d],
            recv_sem=recv.at[d],
            device_id={"tensor": other},
            device_id_type=MESH,
        )
        for d, other in enumerate(peers)
    ]

    def share():
        pl.semaphore_wait(pltpu.get_barrier_semaphore(), n - 1)
        for copy in copies:
            copy.start()

    @pl.when(j == 0)
    def _():
        barrier = pltpu.get_barrier_semaphore()
        for other in peers:
            pl.semaphore_signal(barrier, inc=1, device_id={"tensor": other}, device_id_type=MESH)
        if not plan:
            whole = pltpu.make_async_copy(sources[0], held, sems.at[0])
            whole.start()
            whole.wait()
        for phase in range(2):
            for i, (step, flip) in enumerate(plan):
                at = me // 2 + step
                side = lax.rem(me, 2)
                side = 1 - side if flip else side

                @pl.when((at >= 0) & (at < n // 2))
                def _():
                    index = jnp.clip(2 * at + side, 0, n - 1)
                    copy = pltpu.make_async_copy(sources[i], held.at[index], sems.at[i])
                    if phase == 0:
                        copy.start()
                    else:
                        copy.wait()

    if plain:

        @pl.when(j == parts)
        def _():
            share()

    total = jnp.dot(held[0], w_ref[pl.ds(0, depth), :], preferred_element_type=jnp.float32)
    for d in range(1, n):
        total += jnp.dot(
            held[d], w_ref[pl.ds(d * depth, depth), :], preferred_element_type=jnp.float32
        )

    @pl.when(j < parts)
    def _():
        kept[j] = total
        square = total * total
        part = square[:, :128]
        for c in range(1, tile // 128):
            part = part + square[:, c * 128 : (c + 1) * 128]
        if parts > 1:
            part = part + jnp.where(j == 0, 0.0, lanes[...])
        lanes[...] = part

    @pl.when(j == parts - 1)
    def _():
        mine[...] = lax.dot_general(
            jnp.ones((8, 128), jnp.float32),
            lanes[...],
            (((1,), (1,)), ((), ())),
            precision=lax.Precision.HIGHEST,
            preferred_element_type=jnp.float32,
        )

    if plain:

        @pl.when(j >= parts)
        def _():
            v_ref[...] = total.astype(v_ref.dtype)

    @pl.when(j == last)
    def _():
        if not plain:
            share()
        whole = mine[...]
        for d, copy in enumerate(copies):
            copy.wait()
            whole = whole + got[d]
        sum_ref[...] = whole
        inverse = lax.rsqrt(whole / (n * depth) + EPS)
        pick = (lax.broadcasted_iota(jnp.int32, (8, 128), 0) == 0).astype(jnp.float32)
        column[...] = lax.dot_general(
            inverse,
            pick,
            (((0,), (0,)), ((), ())),
            precision=lax.Precision.HIGHEST,
            preferred_element_type=jnp.float32,
        )
        block = min(128, rows)

        @pl.loop(0, rows // block)
        def _(r):
            at = pl.ds(pl.multiple_of(r * block, block), block)
            cosine, sine, factor = cos_ref[at, :], sin_ref[at, :], column[at, :]
            for h in range(parts * tile // head):
                from_tile, off = divmod(h * head, tile)
                normed = kept[from_tile, at, off : off + head] * factor
                normed = normed * gain_ref[:, h * head : (h + 1) * head]
                turned = normed * cosine + pltpu.roll(normed, head // 2, 1) * sine
                out[at, h * head : (h + 1) * head] = turned.astype(out.dtype)


def project(arrays, plan, weights, gain, cosine, sine, n, first, plain, call):
    rows, depth = arrays[0].shape[-2:]
    width, dloc = weights.shape[1:]
    head = cosine.shape[1]
    tile = min(256, dloc)
    parts = dloc // tile
    dma = pltpu.SemaphoreType.DMA

    def weight_at(j):
        return (first + j // parts, 0, lax.rem(j, parts))

    fixed = lambda j: (0, 0)
    result = jax.ShapeDtypeStruct((rows, dloc), jnp.bfloat16)
    return pl.pallas_call(
        functools.partial(project_kernel, plan=plan, parts=parts, head=head, plain=plain),
        grid=((2 if plain else 1) * parts,),
        in_specs=[pl.BlockSpec(memory_space=pl.ANY)] * len(arrays)
        + [
            pl.BlockSpec((None, width, tile), weight_at),
            pl.BlockSpec((1, dloc), fixed),
            pl.BlockSpec((rows, head), fixed),
            pl.BlockSpec((rows, head), fixed),
        ],
        out_specs=[pl.BlockSpec((rows, dloc), fixed), pl.BlockSpec((8, rows), fixed)]
        + [pl.BlockSpec((rows, tile), lambda j: (0, jnp.maximum(j - parts, 0)))] * plain,
        out_shape=[result, jax.ShapeDtypeStruct((8, rows), jnp.float32)] + [result] * plain,
        scratch_shapes=[
            pltpu.VMEM((n, rows, depth), jnp.bfloat16),
            pltpu.VMEM((parts, rows, tile), jnp.float32),
            pltpu.VMEM((rows, 128), jnp.float32),
            pltpu.VMEM((8, rows), jnp.float32),
            pltpu.VMEM((n - 1, 8, rows), jnp.float32),
            pltpu.VMEM((rows, 128), jnp.float32),
            dma((len(arrays),)),
            dma((n - 1,)),
            dma((n - 1,)),
        ],
        compiler_params=pltpu.CompilerParams(
            dimension_semantics=("arbitrary",),
            vmem_limit_bytes=48 * 1024 * 1024,
            collective_id=call,
            has_side_effects=True,
        ),
        cost_estimate=pl.CostEstimate(
            flops=2 * (1 + plain) * rows * width * dloc,
            bytes_accessed=2 * width * (rows + 3 * dloc) + 10 * rows * dloc,
            transcendentals=0,
        ),
    )(*arrays, weights, gain, cosine, sine)


def combine_kernel(where_ref, kept_ref, other_ref, w_ref, *refs, blocks):
    rows_in, outs, whole = refs[:blocks], refs[blocks:-1], refs[-1]
    d = pl.program_id(0)
    share = rows_in[0].shape[0]
    dloc = w_ref.shape[1]

    @pl.when(d == 0)
    def _():
        for j, piece in enumerate(rows_in):
            start = pl.multiple_of((where_ref[2] ^ j) * share, share)
            whole[pl.ds(start, share), :] = piece[...]

    columns = pl.ds(pl.multiple_of((where_ref[0] ^ d) * dloc, dloc), dloc)
    total = jnp.dot(kept_ref[...], w_ref[...], preferred_element_type=jnp.float32)
    total += jnp.dot(other_ref[...], whole[:, columns], preferred_element_type=jnp.float32)
    for k, out in enumerate(outs):

        @pl.when(d == k)
        def _():
            out[...] = total.astype(out.dtype)


def combine(where, attended, other, w_out, rows_in, n):
    half, dloc = other.shape
    width = w_out.shape[1]
    share = rows_in[0].shape[0]
    return pl.pallas_call(
        functools.partial(combine_kernel, blocks=len(rows_in)),
        grid_spec=pltpu.PrefetchScalarGridSpec(
            num_scalar_prefetch=1,
            grid=(n,),
            in_specs=[
                pl.BlockSpec((half, dloc), lambda d, w: (w[1], 0)),
                pl.BlockSpec((half, dloc), lambda d, w: (0, 0)),
                pl.BlockSpec((dloc, dloc), lambda d, w: (0, w[0] ^ d)),
            ]
            + [pl.BlockSpec((share, width), lambda d, w: (0, 0))] * len(rows_in),
            out_specs=[pl.BlockSpec((half, dloc), lambda d, w: (0, 0))] * n,
            scratch_shapes=[pltpu.VMEM((dloc, width), w_out.dtype)],
        ),
        out_shape=[jax.ShapeDtypeStruct((half, dloc), jnp.bfloat16)] * n,
        compiler_params=pltpu.CompilerParams(
            dimension_semantics=("arbitrary",), vmem_limit_bytes=40 * 1024 * 1024
        ),
        cost_estimate=pl.CostEstimate(
            flops=4 * half * dloc * width,
            bytes_accessed=4 * half * width + 4 * dloc * width,
            transcendentals=0,
        ),
    )(where, attended, other, w_out, *rows_in)


def shards(tokens, w_qkv, q_gain, k_gain, w_out):
    seqs, tok, _ = tokens.shape
    width = w_qkv.shape[0]
    head = width // HEADS
    n = lax.axis_size("tensor")
    count = lax.axis_size("seq")
    here = lax.axis_index("tensor")
    own_index = lax.axis_index("seq")
    hops = [zd for zd in range(n - 2, 0, -2)]
    half = tok // 2
    side = (here // 2) % 2

    def block_of(array, index, size, dim):
        return lax.dynamic_slice_in_dim(array, index * size, size, dim)

    whole, own, up, down = gather_first(tokens, n)
    rest = gather_rest(own, up, down, n)
    step = next(rest)
    weights = jnp.transpose(w_qkv, (1, 0, 2))
    where = jnp.stack([here, side, own_index]).astype(jnp.int32)
    share = width // n // count
    sent = swapped(block_of(w_out, own_index, share, 0), "tensor", 2)
    far = swapped(sent, "seq", 2)
    rows_in = [sent, swapped(sent, "seq", 1), far, swapped(far, "seq", 1)]

    q_index = own_index * tok + jnp.arange(tok, dtype=jnp.int32)
    cosine, sine = rope_tables(q_index.astype(jnp.float32), head)
    chip = own_index // 2
    outer_flags = [(chip >= d).astype(jnp.int32) for d in range(1, count // 2)]
    use = jnp.stack([jnp.int32(1), (own_index % 2).astype(jnp.int32)] + outer_flags + outer_flags)
    scale = head ** (-0.5)
    q_factor = (q_gain * (scale * LOG2E))[None]
    k_factor = k_gain[None]

    mixed, tops, inverses = [], [], []
    for s in range(seqs):
        if s == 0:
            arrays, plan = [whole], []
        else:
            weights, attended = lax.optimization_barrier((weights, attended))
            arrays, plan = [piece[0] for piece in step], [piece[1:] for piece in step]
        k_ready, k_sum, value = project(
            arrays, plan, weights, k_factor, cosine, sine, n, 1, True, 1 + 2 * s
        )
        if s == 0:
            *held, k_sum = lax.optimization_barrier((*step, k_sum))
            step = rest.send(tuple(held))
            while isinstance(step, tuple):
                step = rest.send(step)
        keys = earlier_blocks(k_ready, count, 2)
        values = earlier_blocks(value, count, 2)
        q_ready, q_sum = project(
            arrays, plan, weights, q_factor, cosine, sine, n, 0, False, 2 + 2 * s
        )
        inverses.append(lax.rsqrt(jnp.stack([q_sum[0], k_sum[0]]) / width + EPS))
        attended, top = flash(q_ready, keys, values, use, head)
        tops.append(jnp.max(top, axis=(1, 2)))
        other = swapped(block_of(attended, 1 - side, half, 0), "tensor", 2)
        blocks = combine(where, attended, other, w_out, rows_in, n)
        sums, before = {}, None
        for zd in hops + [0]:
            near = swapped(blocks[zd ^ 1], "tensor", 1)
            if before is not None:
                near, _ = lax.optimization_barrier((near, before))
            sums[zd] = blocks[zd].astype(jnp.float32) + near.astype(jnp.float32)
            if zd:
                sums[zd] = before = sums[zd].astype(jnp.bfloat16)
        same, cross = sums[0], None
        for zd in hops:
            got = swapped(sums[zd], "tensor", zd).astype(jnp.float32)
            if zd & 2:
                cross = got if cross is None else cross + got
            else:
                same = same + got
        first = jnp.where(side == 0, same, cross).astype(jnp.bfloat16)
        second = jnp.where(side == 0, cross, same).astype(jnp.bfloat16)
        mixed.append(jnp.concatenate([first, second], 0))
    top = functools.reduce(jnp.maximum, tops)
    bit = 1
    while bit < count:
        top = jnp.maximum(top, swapped(top, "seq", bit))
        bit *= 2
    peak = top * (1.0 / LOG2E)
    return (jnp.stack(mixed), peak, jnp.stack(inverses, 1))


def solution(mesh):
    return jax.shard_map(
        shards,
        mesh=mesh,
        in_specs=(
            P(None, "seq", "tensor"),
            P(None, None, "tensor"),
            P("tensor"),
            P("tensor"),
            P("tensor", None),
        ),
        out_specs=(P(None, "seq", "tensor"), P("tensor"), P(None, None, "seq")),
        check_vma=False,
    )
```

profile of v0, /device:TPU:11, one launch (start us, length us, event | category | flops | bytes accessed | tf_op | source)
XLA Modules:
  0.0 519.7 jit_solution(4426844652152348701)
XLA Ops:
  0.7 95.3 %shard_map.76 = (bf16[8,1024,512]{2,1,0:T(8,128)(2,1)}, bf16[1024,512]{1,0:T(8,128)(2,1)}, bf16[1024,512]{1,0:T(8,128)(2,1)}, bf16[1024,512]{1,0:T(8,128)(2,1)}) custom-call(bf16[2,1024,512]{2,1,0:T(8,128)(2,1)} %tok_ref.1), custom_call_target="tpu_custom_call" | custom-call | flops 89999998976 | bytes 8388608 | tf_op jit(solution)/shard_map/pallas_call | solution.py:262
  96.0 1.9 fusion
  98.3 17.8 %shard_map.78 = (bf16[1024,512]{1,0:T(8,128)(2,1)S(1)}, f32[8,1024]{1,0:T(8,128)S(1)}, bf16[1024,512]{1,0:T(8,128)(2,1)S(1)}) custom-call(bf16[8,1024,512]{2,1,0:T(8,128)(2,1)} %get-tuple-element.47.refs_0_, bf16[3,4096,512]{2,1,0:T(8,128)(2,1)} %bitcast.24, f32[1,512]{1,0:T(1,128)S(1)} %bitcast.22, f32[1024,128]{1,0:T(8,128)S(1)} %get-tuple-element.98.refs_3_.refs_16_, ...), custom_call_target="tpu_custom_call" | custom-call | flops 8589934592 | bytes 26214400 | tf_op jit(solution)/shard_map/pallas_call | solution.py:457
  116.1 1.3 collective-permute-start.1
  117.4 1.3 collective-permute-start.4
  118.7 2.4 collective-permute-start
  123.1 3.4 collective-permute-start.19
  126.5 14.0 %collective-permute-done.1.refs_2_ = bf16[1024,512]{1,0:T(8,128)(2,1)} collective-permute-done((bf16[1024,512]{1,0:T(8,128)(2,1)S(1)}, bf16[1024,512]{1,0:T(8,128)(2,1)}, u32[]{:S(2)}, u32[]{:S(2)}) %collective-permute-start.1) | collective-permute-done | bytes 1048608 | tf_op jit(solution)/shard_map/ppermute | solution.py:119
  140.5 1.9 collective-permute-start.20
  142.4 20.6 %collective-permute-done.4.refs_6_ = bf16[1024,512]{1,0:T(8,128)(2,1)} collective-permute-done((bf16[1024,512]{1,0:T(8,128)(2,1)S(1)}, bf16[1024,512]{1,0:T(8,128)(2,1)}, u32[]{:S(2)}, u32[]{:S(2)}) %collective-permute-start.4) | collective-permute-done | bytes 1048608 | tf_op jit(solution)/shard_map/ppermute | solution.py:119
  162.9 2.3 collective-permute-start.21
  166.2 1.9 collective-permute-start.22
  169.9 2.3 constant_dynamic-slice_fusion.1
  172.2 4.6 collective-permute-start.2
  176.8 6.4 %collective-permute-done.21.refs_6_ = bf16[1024,512]{1,0:T(8,128)(2,1)} collective-permute-done((bf16[1024,512]{1,0:T(8,128)(2,1)S(1)}, bf16[1024,512]{1,0:T(8,128)(2,1)}, u32[]{:S(2)}, u32[]{:S(2)}) %collective-permute-start.21) | collective-permute-done | bytes 1048608 | tf_op jit(solution)/shard_map/ppermute | solution.py:283
  183.2 4.4 collective-permute-start.5
  187.6 1.8 collective-permute-done.22.refs_7_
  189.3 1.7 collective-permute-start.25
  191.8 2.4 collective-permute-start.26
  194.3 44.1 %shard_map.77 = (bf16[1024,512]{1,0:T(8,128)(2,1)S(1)}, f32[8,1024]{1,0:T(8,128)S(1)}) custom-call(bf16[8,1024,512]{2,1,0:T(8,128)(2,1)} %get-tuple-element.47.refs_0_, bf16[3,4096,512]{2,1,0:T(8,128)(2,1)} %bitcast.25, f32[1,512]{1,0:T(1,128)S(1)} %bitcast.20, f32[1024,128]{1,0:T(8,128)S(1)} %get-tuple-element.98.refs_3_.refs_16_, ...), custom_call_target="tpu_custom_call" | custom-call | flops 4294967296 | bytes 26214400 | tf_op jit(solution)/shard_map/pallas_call | solution.py:457
  239.2 2.2 collective-permute-start.24
  245.3 29.8 %shard_map.79 = (bf16[1024,512]{1,0:T(8,128)(2,1)S(1)}, f32[4,8,128]{2,1,0:T(8,128)S(1)}) custom-call(s32[4]{0:T(128)S(1)} %pad_add_fusion.1.use_ref, bf16[1024,512]{1,0:T(8,128)(2,1)S(1)} %get-tuple-element.48.q_ref, bf16[1024,512]{1,0:T(8,128)(2,1)S(1)} %copy-done.6, bf16[1024,512]{1,0:T(8,128)(2,1)S(1)} %copy-done.10, ...), custom_call_target="tpu_custom_call" | custom-call | flops 17179869184 | bytes 8388608 | tf_op jit(solution)/shard_map/pallas_call | solution.py:84
  277.8 25.1 %shard_map.82 = (bf16[1024,512]{1,0:T(8,128)(2,1)}, f32[8,1024]{1,0:T(8,128)S(1)}, bf16[1024,512]{1,0:T(8,128)(2,1)}) custom-call(bf16[1024,512]{1,0:T(8,128)(2,1)S(1)} %copy-done, bf16[1024,512]{1,0:T(8,128)(2,1)} %collective-permute-done.18.refs_1_, bf16[1024,512]{1,0:T(8,128)(2,1)} %get-tuple-element.67.refs_2_, ...), custom_call_target="tpu_custom_call" | custom-call | flops 8589934592 | bytes 26214400 | tf_op jit(solution)/shard_map/pallas_call | solution.py:457
  305.5 6.2 %collective-permute-start.10 = (bf16[128,4096]{1,0:T(8,128)(2,1)}, bf16[128,4096]{1,0:T(8,128)(2,1)}, u32[]{:S(2)}, u32[]{:S(2)}) collective-permute-start(bf16[128,4096]{1,0:T(8,128)(2,1)} %collective-permute-done.9.refs_2_), channel_id=1, source_target_pairs={{0,8},{8,0},{16,24},{24,16},{1,9},{9,1},{17,25},{25,17},{2,10},{10... | collective-permute-start | bytes 3145736 | tf_op jit(solution)/shard_map/ppermute | solution.py:114
  311.7 1.6 collective-permute-start.6
  313.7 11.7 %collective-permute-done.6.other_ref = bf16[512,512]{1,0:T(8,128)(2,1)S(1)} collective-permute-done((bf16[512,512]{1,0:T(8,128)(2,1)S(1)}, bf16[512,512]{1,0:T(8,128)(2,1)S(1)}, u32[]{:S(2)}, u32[]{:S(2)}) %collective-permute-start.6) | collective-permute-done | bytes 524320 | tf_op jit(solution)/shard_map/ppermute | solution.py:114
  327.0 10.2 %collective-permute-start.31 = (bf16[1024,512]{1,0:T(8,128)(2,1)}, bf16[1024,512]{1,0:T(8,128)(2,1)}, u32[]{:S(2)}, u32[]{:S(2)}) collective-permute-start(bf16[1024,512]{1,0:T(8,128)(2,1)} %collective-permute-done.30.refs_2_), channel_id=1, source_target_pairs={{0,8},{8,0},{16,24},{24,16},{1,9},{9,1},{17,25},{25,17},{2,10},{10... | collective-permute-start | bytes 3145736 | tf_op jit(solution)/shard_map/ppermute | solution.py:114
  337.2 9.0 %collective-permute-done.33.refs_6_ = bf16[1024,512]{1,0:T(8,128)(2,1)} collective-permute-done((bf16[1024,512]{1,0:T(8,128)(2,1)}, bf16[1024,512]{1,0:T(8,128)(2,1)}, u32[]{:S(2)}, u32[]{:S(2)}) %collective-permute-start.33) | collective-permute-done | bytes 1048608 | tf_op jit(solution)/shard_map/ppermute | solution.py:119
  346.2 7.0 %collective-permute-start.34 = (bf16[1024,512]{1,0:T(8,128)(2,1)}, bf16[1024,512]{1,0:T(8,128)(2,1)}, u32[]{:S(2)}, u32[]{:S(2)}) collective-permute-start(bf16[1024,512]{1,0:T(8,128)(2,1)} %collective-permute-done.33.refs_6_), channel_id=1, source_target_pairs={{0,8},{8,0},{16,24},{24,16},{1,9},{9,1},{17,25},{25,17},{2,10},{10... | collective-permute-start | bytes 3145736 | tf_op jit(solution)/shard_map/ppermute | solution.py:114
  353.3 2.3 copy-done.3
  356.6 10.1 %shard_map.80 = (bf16[512,512]{1,0:T(8,128)(2,1)S(1)}, bf16[512,512]{1,0:T(8,128)(2,1)S(1)}, bf16[512,512]{1,0:T(8,128)(2,1)S(1)}, bf16[512,512]{1,0:T(8,128)(2,...) custom-call(s32[3]{0:T(128)S(1)} %pad_add_fusion.where_ref, ...), custom_call_target="tpu_custom_call" | custom-call | flops 4294967296 | bytes 16777216 | tf_op jit(solution)/shard_map/pallas_call | solution.py:521
  367.4 18.5 %shard_map.81 = (bf16[1024,512]{1,0:T(8,128)(2,1)S(1)}, f32[8,1024]{1,0:T(8,128)S(1)}) custom-call(bf16[1024,512]{1,0:T(8,128)(2,1)S(1)} %copy-done, bf16[1024,512]{1,0:T(8,128)(2,1)} %collective-permute-done.18.refs_1_, bf16[1024,512]{1,0:T(8,128)(2,1)S(1)} %copy-done.2, bf16[1024,512]{1,0:T(8,128)(2,1)} %get-tuple-element.68.refs_3_, ...), custom_call_target="tpu_custom_call" | custom-call | flops 4294967296 | bytes 26214400 | tf_op jit(solution)/shard_map/pallas_call | solution.py:457
  385.9 2.5 collective-permute-start.13
  388.5 30.0 %shard_map.83 = (bf16[1024,512]{1,0:T(8,128)(2,1)S(1)}, f32[4,8,128]{2,1,0:T(8,128)S(1)}) custom-call(s32[4]{0:T(128)S(1)} %pad_add_fusion.1.use_ref, bf16[1024,512]{1,0:T(8,128)(2,1)S(1)} %get-tuple-element.70.q_ref, bf16[1024,512]{1,0:T(8,128)(2,1)} %get-tuple-element.71.refs_0_, bf16[1024,512]{1,0:T(8,128)(2,1)} %collective-permute-done.29.refs_1_, ...), custom_call_target="tpu_custom_call" | custom-call | flops 17179869184 | bytes 8388608 | tf_op jit(solution)/shard_map/pallas_call | solution.py:84
  421.1 2.5 collective-permute-start.16
  423.6 9.0 %collective-permute-done.35.other_ref = bf16[512,512]{1,0:T(8,128)(2,1)S(1)} collective-permute-done((bf16[512,512]{1,0:T(8,128)(2,1)S(1)}, bf16[512,512]{1,0:T(8,128)(2,1)S(1)}, u32[]{:S(2)}, u32[]{:S(2)}) %collective-permute-start.35) | collective-permute-done | bytes 524320 | tf_op jit(solution)/shard_map/ppermute | solution.py:114
  432.5 10.1 %shard_map.84 = (bf16[512,512]{1,0:T(8,128)(2,1)S(1)}, bf16[512,512]{1,0:T(8,128)(2,1)S(1)}, bf16[512,512]{1,0:T(8,128)(2,1)S(1)}, bf16[512,512]{1,0:T(8,128)(2,...) custom-call(s32[3]{0:T(128)S(1)} %pad_add_fusion.where_ref, ...), custom_call_target="tpu_custom_call" | custom-call | flops 4294967296 | bytes 16777216 | tf_op jit(solution)/shard_map/pallas_call | solution.py:521
  442.9 7.4 %collective-permute-start.15 = (bf16[512,512]{1,0:T(8,128)(2,1)S(1)}, bf16[512,512]{1,0:T(8,128)(2,1)S(1)}, u32[]{:S(2)}, u32[]{:S(2)}) collective-permute-start(bf16[512,512]{1,0:T(8,128)(2,1)S(1)} %add_convert_fusion.4), channel_id=1, source_target_pairs={{0,4},{1,5},{2,6},{3,7},{4,0},{5,1},{6,2},{7,3},{8,12},{9,13},{10,... | collective-permute-start | bytes 1572872 | tf_op jit(solution)/shard_map/ppermute | solution.py:114
  450.3 1.4 collective-permute-start.38
  452.0 4.7 collective-permute-done.39
  457.6 10.4 %collective-permute-done.38 = bf16[512,512]{1,0:T(8,128)(2,1)S(1)} collective-permute-done((bf16[512,512]{1,0:T(8,128)(2,1)S(1)}, bf16[512,512]{1,0:T(8,128)(2,1)S(1)}, u32[]{:S(2)}, u32[]{:S(2)}) %collective-permute-start.38) | collective-permute-done | bytes 524320 | tf_op jit(solution)/shard_map/ppermute | solution.py:114
  469.0 9.2 %collective-permute-done.37 = bf16[512,512]{1,0:T(8,128)(2,1)S(1)} collective-permute-done((bf16[512,512]{1,0:T(8,128)(2,1)S(1)}, bf16[512,512]{1,0:T(8,128)(2,1)S(1)}, u32[]{:S(2)}, u32[]{:S(2)}) %collective-permute-start.37) | collective-permute-done | bytes 524320 | tf_op jit(solution)/shard_map/ppermute | solution.py:114
  478.2 2.5 collective-permute-start.40
  484.0 2.4 collective-permute-done.44
  486.9 21.1 %collective-permute-done.42 = bf16[512,512]{1,0:T(8,128)(2,1)} collective-permute-done((bf16[512,512]{1,0:T(8,128)(2,1)S(1)}, bf16[512,512]{1,0:T(8,128)(2,1)}, u32[]{:S(2)}, u32[]{:S(2)}) %collective-permute-start.42) | collective-permute-done | bytes 524320 | tf_op jit(solution)/shard_map/ppermute | solution.py:114
  508.0 8.2 %collective-permute-done.41 = bf16[512,512]{1,0:T(8,128)(2,1)} collective-permute-done((bf16[512,512]{1,0:T(8,128)(2,1)}, bf16[512,512]{1,0:T(8,128)(2,1)}, u32[]{:S(2)}, u32[]{:S(2)}) %collective-permute-start.41) | collective-permute-done | bytes 524320 | tf_op jit(solution)/shard_map/ppermute | solution.py:114
  516.3 1.9 select_convert_fusion.1
  518.2 1.5 pad_maximum_fusion
  (130 shorter events, 28.5 us)
Async XLA Ops:
  98.3 70.9 %copy-start = (bf16[1024,512]{1,0:T(8,128)(2,1)S(1)}, bf16[1024,512]{1,0:T(8,128)(2,1)}, u32[]{:S(2)}) copy-start(bf16[1024,512]{1,0:T(8,128)(2,1)} %get-tuple-element.63.refs_0_) | copy-start | bytes 3145732
  116.1 78.2 %copy-start.22 = (f32[512]{0:T(512)S(1)}, f32[512]{0:T(512)}, u32[]{:S(2)}) copy-start(f32[512]{0:T(512)} %param.7) | copy-start | bytes 6148
  116.1 24.4 %collective-permute-start.1 = (bf16[1024,512]{1,0:T(8,128)(2,1)S(1)}, bf16[1024,512]{1,0:T(8,128)(2,1)}, u32[]{:S(2)}, u32[]{:S(2)}) collective-permute-start(bf16[1024,512]{1,0:T(8,128)(2,1)S(1)} %get-tuple-element.49.refs_0_), channel_id=1, source_target_pairs={{0,16},{8,24},{1,17},{9,25},{2,18},{10,26},{3,19},{11,27},{4,20},{... | collective-permute-start | bytes 3145736 | tf_op jit(solution)/shard_map/ppermute | solution.py:119
  117.4 45.5 %collective-permute-start.4 = (bf16[1024,512]{1,0:T(8,128)(2,1)S(1)}, bf16[1024,512]{1,0:T(8,128)(2,1)}, u32[]{:S(2)}, u32[]{:S(2)}) collective-permute-start(bf16[1024,512]{1,0:T(8,128)(2,1)S(1)} %get-tuple-element.50.refs_4_), channel_id=1, source_target_pairs={{0,16},{8,24},{1,17},{9,25},{2,18},{10,26},{3,19},{11,27},{4,20},{... | collective-permute-start | bytes 3145736 | tf_op jit(solution)/shard_map/ppermute | solution.py:119
  118.7 46.5 %collective-permute-start = (bf16[1024,512]{1,0:T(8,128)(2,1)S(1)}, bf16[1024,512]{1,0:T(8,128)(2,1)S(1)}, u32[]{:S(2)}, u32[]{:S(2)}) collective-permute-start(bf16[1024,512]{1,0:T(8,128)(2,1)S(1)} %get-tuple-element.49.refs_0_), channel_id=1, source_target_pairs={{0,8},{8,0},{16,24},{24,16},{1,9},{9,1},{17,25},{25,17},{2,10},{10... | collective-permute-start | bytes 3145736 | tf_op jit(solution)/shard_map/ppermute | solution.py:114
  122.1 46.0 %collective-permute-start.3 = (bf16[1024,512]{1,0:T(8,128)(2,1)S(1)}, bf16[1024,512]{1,0:T(8,128)(2,1)S(1)}, u32[]{:S(2)}, u32[]{:S(2)}) collective-permute-start(bf16[1024,512]{1,0:T(8,128)(2,1)S(1)} %get-tuple-element.50.refs_4_), channel_id=1, source_target_pairs={{0,8},{8,0},{16,24},{24,16},{1,9},{9,1},{17,25},{25,17},{2,10},{10... | collective-permute-start | bytes 3145736 | tf_op jit(solution)/shard_map/ppermute | solution.py:114
  123.1 49.1 %collective-permute-start.19 = (bf16[1024,512]{1,0:T(8,128)(2,1)S(1)}, bf16[1024,512]{1,0:T(8,128)(2,1)}, u32[]{:S(2)}, u32[]{:S(2)}) collective-permute-start(bf16[1024,512]{1,0:T(8,128)(2,1)S(1)} %copy-done.1), channel_id=1, source_target_pairs={{2,3},{3,2},{4,5},{5,4},{6,7},{7,6},{10,11},{11,10},{12,13},{13,12... | collective-permute-start | bytes 3145736 | tf_op jit(solution)/shard_map/ppermute | solution.py:283
  140.5 31.8 %collective-permute-start.20 = (bf16[1024,512]{1,0:T(8,128)(2,1)}, bf16[1024,512]{1,0:T(8,128)(2,1)}, u32[]{:S(2)}, u32[]{:S(2)}) collective-permute-start(bf16[1024,512]{1,0:T(8,128)(2,1)} %get-tuple-element.68.refs_3_), channel_id=1, source_target_pairs={{0,1},{1,0},{2,3},{3,2},{4,5},{5,4},{8,9},{9,8},{10,11},{11,10},{1... | collective-permute-start | bytes 3145736 | tf_op jit(solution)/shard_map/ppermute | solution.py:283
  162.9 20.3 %collective-permute-start.21 = (bf16[1024,512]{1,0:T(8,128)(2,1)S(1)}, bf16[1024,512]{1,0:T(8,128)(2,1)}, u32[]{:S(2)}, u32[]{:S(2)}) collective-permute-start(bf16[1024,512]{1,0:T(8,128)(2,1)S(1)} %copy-done.1), channel_id=1, source_target_pairs={{2,4},{3,5},{4,6},{5,7},{10,12},{11,13},{12,14},{13,15},{18,20},{1... | collective-permute-start | bytes 3145736 | tf_op jit(solution)/shard_map/ppermute | solution.py:283
  166.2 23.1 %collective-permute-start.22 = (bf16[1024,512]{1,0:T(8,128)(2,1)}, bf16[1024,512]{1,0:T(8,128)(2,1)}, u32[]{:S(2)}, u32[]{:S(2)}) collective-permute-start(bf16[1024,512]{1,0:T(8,128)(2,1)} %get-tuple-element.68.refs_3_), channel_id=1, source_target_pairs={{2,0},{3,1},{4,2},{5,3},{10,8},{11,9},{12,10},{13,11},{18,16},{19,... | collective-permute-start | bytes 3145736 | tf_op jit(solution)/shard_map/ppermute | solution.py:283
  169.2 22.6 %collective-permute-start.18 = (bf16[1024,512]{1,0:T(8,128)(2,1)S(1)}, bf16[1024,512]{1,0:T(8,128)(2,1)}, u32[]{:S(2)}, u32[]{:S(2)}) collective-permute-start(bf16[1024,512]{1,0:T(8,128)(2,1)S(1)} %copy-done), channel_id=1, source_target_pairs={{0,1},{1,0},{2,3},{3,2},{4,5},{5,4},{6,7},{7,6},{8,9},{9,8},{10,11... | collective-permute-start | bytes 3145736 | tf_op jit(solution)/shard_map/ppermute | solution.py:283
  172.2 66.2 %collective-permute-start.7 = (bf16[128,4096]{1,0:T(8,128)(2,1)}, bf16[128,4096]{1,0:T(8,128)(2,1)}, u32[]{:S(2)}, u32[]{:S(2)}) collective-permute-start(bf16[128,4096]{1,0:T(8,128)(2,1)} %constant_dynamic-slice_fusion.1), channel_id=1, source_target_pairs={{0,2},{1,3},{2,0},{3,1},{4,6},{5,7},{6,4},{7,5},{8,10},{9,11},{10,... | collective-permute-start | bytes 3145736 | tf_op jit(solution)/shard_map/ppermute | solution.py:114
  172.2 66.9 %collective-permute-start.2 = (bf16[1024,512]{1,0:T(8,128)(2,1)}, bf16[1024,512]{1,0:T(8,128)(2,1)}, u32[]{:S(2)}, u32[]{:S(2)}) collective-permute-start(bf16[1024,512]{1,0:T(8,128)(2,1)} %collective-permute-done.1.refs_2_), channel_id=1, source_target_pairs={{0,8},{8,0},{16,24},{24,16},{1,9},{9,1},{17,25},{25,17},{2,10},{10... | collective-permute-start | bytes 3145736 | tf_op jit(solution)/shard_map/ppermute | solution.py:114
  183.2 58.2 %collective-permute-start.5 = (bf16[1024,512]{1,0:T(8,128)(2,1)}, bf16[1024,512]{1,0:T(8,128)(2,1)S(1)}, u32[]{:S(2)}, u32[]{:S(2)}) collective-permute-start(bf16[1024,512]{1,0:T(8,128)(2,1)} %collective-permute-done.4.refs_6_), channel_id=1, source_target_pairs={{0,8},{8,0},{16,24},{24,16},{1,9},{9,1},{17,25},{25,17},{2,10},{10... | collective-permute-start | bytes 3145736 | tf_op jit(solution)/shard_map/ppermute | solution.py:114
  189.3 53.0 %collective-permute-start.25 = (bf16[1024,512]{1,0:T(8,128)(2,1)}, bf16[1024,512]{1,0:T(8,128)(2,1)}, u32[]{:S(2)}, u32[]{:S(2)}) collective-permute-start(bf16[1024,512]{1,0:T(8,128)(2,1)} %collective-permute-done.21.refs_6_), channel_id=1, source_target_pairs={{4,6},{5,7},{12,14},{13,15},{20,22},{21,23},{28,30},{29,31}} | collective-permute-start | bytes 3145736 | tf_op jit(solution)/shard_map/ppermute | solution.py:283
  191.8 51.3 %collective-permute-start.26 = (bf16[1024,512]{1,0:T(8,128)(2,1)}, bf16[1024,512]{1,0:T(8,128)(2,1)}, u32[]{:S(2)}, u32[]{:S(2)}) collective-permute-start(bf16[1024,512]{1,0:T(8,128)(2,1)} %collective-permute-done.22.refs_7_), channel_id=1, source_target_pairs={{2,0},{3,1},{10,8},{11,9},{18,16},{19,17},{26,24},{27,25}} | collective-permute-start | bytes 3145736 | tf_op jit(solution)/shard_map/ppermute | solution.py:283
  194.3 49.8 %copy-start.8 = (bf16[1024,512]{1,0:T(8,128)(2,1)S(1)}, bf16[1024,512]{1,0:T(8,128)(2,1)}, u32[]{:S(2)}) copy-start(bf16[1024,512]{1,0:T(8,128)(2,1)} %copy-done.7) | copy-start | bytes 3145732
  238.4 36.7 %collective-permute-start.23 = (bf16[1024,512]{1,0:T(8,128)(2,1)}, bf16[1024,512]{1,0:T(8,128)(2,1)S(1)}, u32[]{:S(2)}, u32[]{:S(2)}) collective-permute-start(bf16[1024,512]{1,0:T(8,128)(2,1)} %collective-permute-done.21.refs_6_), channel_id=1, source_target_pairs={{4,5},{5,4},{6,7},{7,6},{12,13},{13,12},{14,15},{15,14},{20,21},{2... | collective-permute-start | bytes 3145736 | tf_op jit(solution)/shard_map/ppermute | solution.py:283
  239.2 36.0 %collective-permute-start.24 = (bf16[1024,512]{1,0:T(8,128)(2,1)}, bf16[1024,512]{1,0:T(8,128)(2,1)S(1)}, u32[]{:S(2)}, u32[]{:S(2)}) collective-permute-start(bf16[1024,512]{1,0:T(8,128)(2,1)} %collective-permute-done.22.refs_7_), channel_id=1, source_target_pairs={{0,1},{1,0},{2,3},{3,2},{8,9},{9,8},{10,11},{11,10},{16,17},{17,16... | collective-permute-start | bytes 3145736 | tf_op jit(solution)/shard_map/ppermute | solution.py:283
  242.4 63.1 %collective-permute-start.9 = (bf16[128,4096]{1,0:T(8,128)(2,1)}, bf16[128,4096]{1,0:T(8,128)(2,1)}, u32[]{:S(2)}, u32[]{:S(2)}) collective-permute-start(bf16[128,4096]{1,0:T(8,128)(2,1)} %collective-permute-done.7.refs_0_), channel_id=1, source_target_pairs={{0,16},{8,24},{16,0},{24,8},{1,17},{9,25},{17,1},{25,9},{2,18},{10... | collective-permute-start | bytes 3145736 | tf_op jit(solution)/shard_map/ppermute | solution.py:114
  242.4 32.9 %collective-permute-start.27 = (bf16[1024,512]{1,0:T(8,128)(2,1)}, bf16[1024,512]{1,0:T(8,128)(2,1)S(1)}, u32[]{:S(2)}, u32[]{:S(2)}) collective-permute-start(bf16[1024,512]{1,0:T(8,128)(2,1)} %collective-permute-done.25.refs_10_), channel_id=1, source_target_pairs={{6,7},{7,6},{14,15},{15,14},{22,23},{23,22},{30,31},{31,30}} | collective-permute-start | bytes 3145736 | tf_op jit(solution)/shard_map/ppermute | solution.py:283
  243.1 32.1 %collective-permute-start.28 = (bf16[1024,512]{1,0:T(8,128)(2,1)}, bf16[1024,512]{1,0:T(8,128)(2,1)S(1)}, u32[]{:S(2)}, u32[]{:S(2)}) collective-permute-start(bf16[1024,512]{1,0:T(8,128)(2,1)} %collective-permute-done.26.refs_11_), channel_id=1, source_target_pairs={{0,1},{1,0},{8,9},{9,8},{16,17},{17,16},{24,25},{25,24}} | collective-permute-start | bytes 3145736 | tf_op jit(solution)/shard_map/ppermute | solution.py:283
  275.1 38.2 %collective-permute-start.8 = (bf16[128,4096]{1,0:T(8,128)(2,1)}, bf16[128,4096]{1,0:T(8,128)(2,1)}, u32[]{:S(2)}, u32[]{:S(2)}) collective-permute-start(bf16[128,4096]{1,0:T(8,128)(2,1)} %collective-permute-done.7.refs_0_), channel_id=1, source_target_pairs={{0,8},{8,0},{16,24},{24,16},{1,9},{9,1},{17,25},{25,17},{2,10},{10... | collective-permute-start | bytes 3145736 | tf_op jit(solution)/shard_map/ppermute | solution.py:114
  302.8 24.1 %collective-permute-start.30 = (bf16[1024,512]{1,0:T(8,128)(2,1)}, bf16[1024,512]{1,0:T(8,128)(2,1)}, u32[]{:S(2)}, u32[]{:S(2)}) collective-permute-start(bf16[1024,512]{1,0:T(8,128)(2,1)} %get-tuple-element.71.refs_0_), channel_id=1, source_target_pairs={{0,16},{8,24},{1,17},{9,25},{2,18},{10,26},{3,19},{11,27},{4,20},{... | collective-permute-start | bytes 3145736 | tf_op jit(solution)/shard_map/ppermute | solution.py:119
  304.1 42.0 %collective-permute-start.33 = (bf16[1024,512]{1,0:T(8,128)(2,1)}, bf16[1024,512]{1,0:T(8,128)(2,1)}, u32[]{:S(2)}, u32[]{:S(2)}) collective-permute-start(bf16[1024,512]{1,0:T(8,128)(2,1)} %get-tuple-element.72.refs_4_), channel_id=1, source_target_pairs={{0,16},{8,24},{1,17},{9,25},{2,18},{10,26},{3,19},{11,27},{4,20},{... | collective-permute-start | bytes 3145736 | tf_op jit(solution)/shard_map/ppermute | solution.py:119
  305.5 47.8 %collective-permute-start.10 = (bf16[128,4096]{1,0:T(8,128)(2,1)}, bf16[128,4096]{1,0:T(8,128)(2,1)}, u32[]{:S(2)}, u32[]{:S(2)}) collective-permute-start(bf16[128,4096]{1,0:T(8,128)(2,1)} %collective-permute-done.9.refs_2_), channel_id=1, source_target_pairs={{0,8},{8,0},{16,24},{24,16},{1,9},{9,1},{17,25},{25,17},{2,10},{10... | collective-permute-start | bytes 3145736 | tf_op jit(solution)/shard_map/ppermute | solution.py:114
  311.7 13.8 %collective-permute-start.6 = (bf16[512,512]{1,0:T(8,128)(2,1)S(1)}, bf16[512,512]{1,0:T(8,128)(2,1)S(1)}, u32[]{:S(2)}, u32[]{:S(2)}) collective-permute-start(bf16[512,512]{1,0:T(8,128)(2,1)S(1)} %constant_dynamic-slice_fusion.2), channel_id=1, source_target_pairs={{0,2},{1,3},{2,0},{3,1},{4,6},{5,7},{6,4},{7,5},{8,10},{9,11},{10,... | collective-permute-start | bytes 1572872 | tf_op jit(solution)/shard_map/ppermute | solution.py:114
  313.3 72.6 %collective-permute-start.29 = (bf16[1024,512]{1,0:T(8,128)(2,1)}, bf16[1024,512]{1,0:T(8,128)(2,1)}, u32[]{:S(2)}, u32[]{:S(2)}) collective-permute-start(bf16[1024,512]{1,0:T(8,128)(2,1)} %get-tuple-element.71.refs_0_), channel_id=1, source_target_pairs={{0,8},{8,0},{16,24},{24,16},{1,9},{9,1},{17,25},{25,17},{2,10},{10... | collective-permute-start | bytes 3145736 | tf_op jit(solution)/shard_map/ppermute | solution.py:114
  326.3 62.2 %collective-permute-start.32 = (bf16[1024,512]{1,0:T(8,128)(2,1)}, bf16[1024,512]{1,0:T(8,128)(2,1)}, u32[]{:S(2)}, u32[]{:S(2)}) collective-permute-start(bf16[1024,512]{1,0:T(8,128)(2,1)} %get-tuple-element.72.refs_4_), channel_id=1, source_target_pairs={{0,8},{8,0},{16,24},{24,16},{1,9},{9,1},{17,25},{25,17},{2,10},{10... | collective-permute-start | bytes 3145736 | tf_op jit(solution)/shard_map/ppermute | solution.py:114
  327.0 61.5 %collective-permute-start.31 = (bf16[1024,512]{1,0:T(8,128)(2,1)}, bf16[1024,512]{1,0:T(8,128)(2,1)}, u32[]{:S(2)}, u32[]{:S(2)}) collective-permute-start(bf16[1024,512]{1,0:T(8,128)(2,1)} %collective-permute-done.30.refs_2_), channel_id=1, source_target_pairs={{0,8},{8,0},{16,24},{24,16},{1,9},{9,1},{17,25},{25,17},{2,10},{10... | collective-permute-start | bytes 3145736 | tf_op jit(solution)/shard_map/ppermute | solution.py:114
  346.2 42.3 %collective-permute-start.34 = (bf16[1024,512]{1,0:T(8,128)(2,1)}, bf16[1024,512]{1,0:T(8,128)(2,1)}, u32[]{:S(2)}, u32[]{:S(2)}) collective-permute-start(bf16[1024,512]{1,0:T(8,128)(2,1)} %collective-permute-done.33.refs_6_), channel_id=1, source_target_pairs={{0,8},{8,0},{16,24},{24,16},{1,9},{9,1},{17,25},{25,17},{2,10},{10... | collective-permute-start | bytes 3145736 | tf_op jit(solution)/shard_map/ppermute | solution.py:114
  366.7 54.3 %collective-permute-start.14 = (bf16[512,512]{1,0:T(8,128)(2,1)S(1)}, bf16[512,512]{1,0:T(8,128)(2,1)S(1)}, u32[]{:S(2)}, u32[]{:S(2)}) collective-permute-start(bf16[512,512]{1,0:T(8,128)(2,1)S(1)} %get-tuple-element.59), channel_id=1, source_target_pairs={{0,1},{1,0},{2,3},{3,2},{4,5},{5,4},{6,7},{7,6},{8,9},{9,8},{10,11... | collective-permute-start | bytes 1572872 | tf_op jit(solution)/shard_map/ppermute | solution.py:114
  385.9 37.6 %collective-permute-start.13 = (bf16[512,512]{1,0:T(8,128)(2,1)S(1)}, bf16[512,512]{1,0:T(8,128)(2,1)S(1)}, u32[]{:S(2)}, u32[]{:S(2)}) collective-permute-start(bf16[512,512]{1,0:T(8,128)(2,1)S(1)} %get-tuple-element.57), channel_id=1, source_target_pairs={{0,1},{1,0},{2,3},{3,2},{4,5},{5,4},{6,7},{7,6},{8,9},{9,8},{10,11... | collective-permute-start | bytes 1572872 | tf_op jit(solution)/shard_map/ppermute | solution.py:114
  418.5 14.0 %collective-permute-start.35 = (bf16[512,512]{1,0:T(8,128)(2,1)S(1)}, bf16[512,512]{1,0:T(8,128)(2,1)S(1)}, u32[]{:S(2)}, u32[]{:S(2)}) collective-permute-start(bf16[512,512]{1,0:T(8,128)(2,1)S(1)} %constant_dynamic-slice_fusion), channel_id=1, source_target_pairs={{0,2},{1,3},{2,0},{3,1},{4,6},{5,7},{6,4},{7,5},{8,10},{9,11},{10,... | collective-permute-start | bytes 1572872 | tf_op jit(solution)/shard_map/ppermute | solution.py:114
  418.8 31.5 %collective-permute-start.12 = (bf16[512,512]{1,0:T(8,128)(2,1)S(1)}, bf16[512,512]{1,0:T(8,128)(2,1)S(1)}, u32[]{:S(2)}, u32[]{:S(2)}) collective-permute-start(bf16[512,512]{1,0:T(8,128)(2,1)S(1)} %get-tuple-element.55), channel_id=1, source_target_pairs={{0,1},{1,0},{2,3},{3,2},{4,5},{5,4},{6,7},{7,6},{8,9},{9,8},{10,11... | collective-permute-start | bytes 1572872 | tf_op jit(solution)/shard_map/ppermute | solution.py:114
  419.2 32.8 %collective-permute-start.11 = (bf16[512,512]{1,0:T(8,128)(2,1)S(1)}, bf16[512,512]{1,0:T(8,128)(2,1)S(1)}, u32[]{:S(2)}, u32[]{:S(2)}) collective-permute-start(bf16[512,512]{1,0:T(8,128)(2,1)S(1)} %get-tuple-element.53), channel_id=1, source_target_pairs={{0,1},{1,0},{2,3},{3,2},{4,5},{5,4},{6,7},{7,6},{8,9},{9,8},{10,11... | collective-permute-start | bytes 1572872 | tf_op jit(solution)/shard_map/ppermute | solution.py:114
  421.1 61.0 %collective-permute-start.16 = (bf16[512,512]{1,0:T(8,128)(2,1)S(1)}, bf16[512,512]{1,0:T(8,128)(2,1)S(1)}, u32[]{:S(2)}, u32[]{:S(2)}) collective-permute-start(bf16[512,512]{1,0:T(8,128)(2,1)S(1)} %add_convert_fusion.5), channel_id=1, source_target_pairs={{0,6},{1,7},{2,4},{3,5},{4,2},{5,3},{6,0},{7,1},{8,14},{9,15},{10,... | collective-permute-start | bytes 1572872 | tf_op jit(solution)/shard_map/ppermute | solution.py:114
  442.7 14.0 %collective-permute-start.39 = (bf16[512,512]{1,0:T(8,128)(2,1)S(1)}, bf16[512,512]{1,0:T(8,128)(2,1)S(1)}, u32[]{:S(2)}, u32[]{:S(2)}) collective-permute-start(bf16[512,512]{1,0:T(8,128)(2,1)S(1)} %get-tuple-element.81), channel_id=1, source_target_pairs={{0,1},{1,0},{2,3},{3,2},{4,5},{5,4},{6,7},{7,6},{8,9},{9,8},{10,11... | collective-permute-start | bytes 1572872 | tf_op jit(solution)/shard_map/ppermute | solution.py:114
  442.9 38.0 %collective-permute-start.15 = (bf16[512,512]{1,0:T(8,128)(2,1)S(1)}, bf16[512,512]{1,0:T(8,128)(2,1)S(1)}, u32[]{:S(2)}, u32[]{:S(2)}) collective-permute-start(bf16[512,512]{1,0:T(8,128)(2,1)S(1)} %add_convert_fusion.4), channel_id=1, source_target_pairs={{0,4},{1,5},{2,6},{3,7},{4,0},{5,1},{6,2},{7,3},{8,12},{9,13},{10,... | collective-permute-start | bytes 1572872 | tf_op jit(solution)/shard_map/ppermute | solution.py:114
  450.3 17.7 %collective-permute-start.38 = (bf16[512,512]{1,0:T(8,128)(2,1)S(1)}, bf16[512,512]{1,0:T(8,128)(2,1)S(1)}, u32[]{:S(2)}, u32[]{:S(2)}) collective-permute-start(bf16[512,512]{1,0:T(8,128)(2,1)S(1)} %get-tuple-element.79), channel_id=1, source_target_pairs={{0,1},{1,0},{2,3},{3,2},{4,5},{5,4},{6,7},{7,6},{8,9},{9,8},{10,11... | collective-permute-start | bytes 1572872 | tf_op jit(solution)/shard_map/ppermute | solution.py:114
  451.9 28.9 %collective-permute-start.17 = (bf16[512,512]{1,0:T(8,128)(2,1)S(1)}, bf16[512,512]{1,0:T(8,128)(2,1)S(1)}, u32[]{:S(2)}, u32[]{:S(2)}) collective-permute-start(bf16[512,512]{1,0:T(8,128)(2,1)S(1)} %add_convert_fusion.3), channel_id=1, source_target_pairs={{0,2},{1,3},{2,0},{3,1},{4,6},{5,7},{6,4},{7,5},{8,10},{9,11},{10,... | collective-permute-start | bytes 1572872 | tf_op jit(solution)/shard_map/ppermute | solution.py:114
  456.7 21.5 %collective-permute-start.37 = (bf16[512,512]{1,0:T(8,128)(2,1)S(1)}, bf16[512,512]{1,0:T(8,128)(2,1)S(1)}, u32[]{:S(2)}, u32[]{:S(2)}) collective-permute-start(bf16[512,512]{1,0:T(8,128)(2,1)S(1)} %get-tuple-element.77), channel_id=1, source_target_pairs={{0,1},{1,0},{2,3},{3,2},{4,5},{5,4},{6,7},{7,6},{8,9},{9,8},{10,11... | collective-permute-start | bytes 1572872 | tf_op jit(solution)/shard_map/ppermute | solution.py:114
  468.0 18.9 %collective-permute-start.36 = (bf16[512,512]{1,0:T(8,128)(2,1)S(1)}, bf16[512,512]{1,0:T(8,128)(2,1)}, u32[]{:S(2)}, u32[]{:S(2)}) collective-permute-start(bf16[512,512]{1,0:T(8,128)(2,1)S(1)} %get-tuple-element.75), channel_id=1, source_target_pairs={{0,1},{1,0},{2,3},{3,2},{4,5},{5,4},{6,7},{7,6},{8,9},{9,8},{10,11... | collective-permute-start | bytes 1572872 | tf_op jit(solution)/shard_map/ppermute | solution.py:114
  478.2 29.8 %collective-permute-start.40 = (bf16[512,512]{1,0:T(8,128)(2,1)}, bf16[512,512]{1,0:T(8,128)(2,1)}, u32[]{:S(2)}, u32[]{:S(2)}) collective-permute-start(bf16[512,512]{1,0:T(8,128)(2,1)} %add_convert_fusion.1), channel_id=1, source_target_pairs={{0,4},{1,5},{2,6},{3,7},{4,0},{5,1},{6,2},{7,3},{8,12},{9,13},{10,... | collective-permute-start | bytes 1572872 | tf_op jit(solution)/shard_map/ppermute | solution.py:114
  480.9 35.4 %collective-permute-start.41 = (bf16[512,512]{1,0:T(8,128)(2,1)}, bf16[512,512]{1,0:T(8,128)(2,1)}, u32[]{:S(2)}, u32[]{:S(2)}) collective-permute-start(bf16[512,512]{1,0:T(8,128)(2,1)} %add_convert_fusion.2), channel_id=1, source_target_pairs={{0,6},{1,7},{2,4},{3,5},{4,2},{5,3},{6,0},{7,1},{8,14},{9,15},{10,... | collective-permute-start | bytes 1572872 | tf_op jit(solution)/shard_map/ppermute | solution.py:114
  481.0 27.1 %collective-permute-start.42 = (bf16[512,512]{1,0:T(8,128)(2,1)S(1)}, bf16[512,512]{1,0:T(8,128)(2,1)}, u32[]{:S(2)}, u32[]{:S(2)}) collective-permute-start(bf16[512,512]{1,0:T(8,128)(2,1)S(1)} %add_convert_fusion), channel_id=1, source_target_pairs={{0,2},{1,3},{2,0},{3,1},{4,6},{5,7},{6,4},{7,5},{8,10},{9,11},{10,... | collective-permute-start | bytes 1572872 | tf_op jit(solution)/shard_map/ppermute | solution.py:114
  482.7 1.2 collective-permute-start.43
  484.0 2.4 collective-permute-start.44
  (20 other events, 249.7 us)
where the time goes:
time: 520 us
  Pallas kernels  281 us (54%)
  waiting for transfers between devices  130 us (25%)
  starting transfers between devices  81.9 us (16%)
  local copies, waits for them, and re-layouts  15.3 us (3%)
  other arithmetic  10.2 us (2%)
    pallas_call x4, Pallas kernels, project(): pl.pallas_call(functools.partial(project_kernel, plan=plan, parts=parts,...  105 us
    pallas_call x1, Pallas kernels, gather_first(): pl.pallas_call(functools.partial(gather_kernel, line=line), in_specs=[pl....  95.3 us
    ppermute x30, waiting for transfers between devices, swapped(): return lax.ppermute(value, axis, [(i, i ^ bit) for i in range(size)])  77.9 us
    pallas_call x2, Pallas kernels, flash(): pl.pallas_call(functools.partial(flash_kernel, blocks=blocks, bq=bq, bk=b...  59.8 us
    ppermute x30, starting transfers between devices, swapped(): return lax.ppermute(value, axis, [(i, i ^ bit) for i in range(size)])  57.9 us
    ppermute x4, waiting for transfers between devices, earlier_blocks(): lax.ppermute(block, 'seq', [(i, i + across * d) for i in range(count - ac...  43.5 us
    pallas_call x2, Pallas kernels, combine(): pl.pallas_call(functools.partial(combine_kernel, blocks=len(rows_in)), gr...  20.2 us
    ppermute x11, starting transfers between devices, moved(): return lax.ppermute(value, 'tensor', pairs)  18.8 us
  transfers between devices with their start and end apart: 45, of which 15 were waited for; matrix products, arithmetic and copies ran while one was open for 1% of the time, Pallas kernels for 32%

commit v1 on v0

--- a/solution.py
+++ b/solution.py
@@ -32,66 +32,79 @@
     k_refs, v_refs = refs[:blocks], refs[blocks : 2 * blocks]
     o_ref, top_ref, m_s, l_s, acc_s = refs[2 * blocks :]
     rows = q_ref.shape[0]
+    turns = rows // bq
+
+    def step(i, k, v, first):
+        at = pl.ds(i * bq, bq)
+        s = lax.dot_general(
+            q_ref[at, :], k, (((1,), (1,)), ((), ())), preferred_element_type=jnp.float32
+        )
+        if first:
+            row = lax.broadcasted_iota(jnp.int32, s.shape, 0)
+            col = lax.broadcasted_iota(jnp.int32, s.shape, 1)
+            s = jnp.where(col <= row, s, NEG)
+        top = jnp.max(s, -1, keepdims=True)
+        if first:
+            m_new = jnp.broadcast_to(top, (bq, 128))
+        else:
+            m_old = m_s[at, :]
+            m_new = jnp.maximum(m_old, top)
+        p = jnp.exp2(s - jnp.tile(m_new, (1, s.shape[1] // 128)))
+        part = p[:, :128]
+        for j in range(1, s.shape[1] // 128):
+            part = part + p[:, j * 128 : (j + 1) * 128]
+        pv = jnp.dot(p.astype(jnp.bfloat16), v, preferred_element_type=jnp.float32)
+        if first:
+            l_s[at, :] = part
+            acc_s[at, :] = pv
+        else:
+            alpha = jnp.exp2(m_old - m_new)
+            l_s[at, :] = l_s[at, :] * alpha + part
+            acc_s[at, :] = acc_s[at, :] * alpha + pv
+        m_s[at, :] = m_new
+
+    for i in range(turns):
+        step(i, k_refs[0][pl.ds(i * bq, bq), :], v_refs[0][pl.ds(i * bq, bq), :], True)
+    for i in range(turns):
+        for j in range(i):
+            step(i, k_refs[0][pl.ds(j * bq, bq), :], v_refs[0][pl.ds(j * bq, bq), :], False)
+    for e in range(1, blocks):
+
+        @pl.when(use_ref[e] > 0)
+        def _():
+            for j in range(rows // bk):
+                for i in range(turns):
+                    step(i, k_refs[e][pl.ds(j * bk, bk), :], v_refs[e][pl.ds(j * bk, bk), :], False)
+
     best = jnp.full((1, 128), NEG, jnp.float32)
-    for i in range(rows // bq):
-        q = q_ref[pl.ds(i * bq, bq), :]
-        m_s[...] = jnp.full(m_s.shape, NEG, jnp.float32)
-        l_s[...] = jnp.zeros(l_s.shape, jnp.float32)
-        acc_s[...] = jnp.zeros(acc_s.shape, jnp.float32)
-
-        def step(k, v, masked):
-            s = lax.dot_general(q, k, (((1,), (1,)), ((), ())), preferred_element_type=jnp.float32)
-            if masked:
-                row = lax.broadcasted_iota(jnp.int32, s.shape, 0)
-                col = lax.broadcasted_iota(jnp.int32, s.shape, 1)
-                s = jnp.where(col <= row, s, NEG)
-            m_old = m_s[...]
-            m_new = jnp.maximum(m_old, jnp.max(s, -1, keepdims=True))
-            p = jnp.exp2(s - jnp.tile(m_new, (1, s.shape[1] // 128)))
-            alpha = jnp.exp2(m_old - m_new)
-            part = p[:, :128]
-            for j in range(1, s.shape[1] // 128):
-                part = part + p[:, j * 128 : (j + 1) * 128]
-            l_s[...] = l_s[...] * alpha + part
-            acc_s[...] = acc_s[...] * alpha + jnp.dot(
-                p.astype(jnp.bfloat16), v, preferred_element_type=jnp.float32
-            )
-            m_s[...] = m_new
-
-        step(k_refs[0][pl.ds(i * bq, bq), :], v_refs[0][pl.ds(i * bq, bq), :], True)
-        for j in range(i):
-            step(k_refs[0][pl.ds(j * bq, bq), :], v_refs[0][pl.ds(j * bq, bq), :], False)
-        for e in range(1, blocks):
-
-            @pl.when(use_ref[e] > 0)
-            def _():
-                for j in range(rows // bk):
-                    step(k_refs[e][pl.ds(j * bk, bk), :], v_refs[e][pl.ds(j * bk, bk), :], False)
-
-        denom = jnp.sum(l_s[...], -1, keepdims=True)
-        o_ref[pl.ds(i * bq, bq), :] = (acc_s[...] / denom).astype(o_ref.dtype)
-        best = jnp.maximum(best, jnp.max(m_s[...], 0, keepdims=True))
+    for i in range(turns):
+        at = pl.ds(i * bq, bq)
+        denom = jnp.sum(l_s[at, :], -1, keepdims=True)
+        o_ref[at, :] = (acc_s[at, :] / denom).astype(o_ref.dtype)
+        best = jnp.maximum(best, jnp.max(m_s[at, :], 0, keepdims=True))
     top_ref[...] = jnp.broadcast_to(best, top_ref.shape)
 
 
-def flash(q, keys, values, use, head):
-    rows, dloc = q.shape
-    heads = dloc // head
-    blocks = len(keys)
+def flash(q, pairs, use, head, first, heads):
+    rows = q.shape[0]
+    dloc = heads * head
+    blocks = len(pairs)
     bq = min(BLOCK_Q, rows)
     bk = min(BLOCK_K, rows)
-    spec = pl.BlockSpec((rows, head), lambda h, f: (0, h))
+    spec = pl.BlockSpec((rows, head), lambda h, f: (0, h + first))
+    made = pl.BlockSpec((rows, head), lambda h, f: (0, h))
+    second = pl.BlockSpec((rows, head), lambda h, f: (0, h + heads))
     return pl.pallas_call(
         functools.partial(flash_kernel, blocks=blocks, bq=bq, bk=bk),
         grid_spec=pltpu.PrefetchScalarGridSpec(
             num_scalar_prefetch=1,
             grid=(heads,),
-            in_specs=[spec] * (1 + 2 * blocks),
-            out_specs=[spec, pl.BlockSpec((None, 8, 128), lambda h, f: (h, 0, 0))],
+            in_specs=[spec] + [made] * blocks + [second] * blocks,
+            out_specs=[made, pl.BlockSpec((None, 8, 128), lambda h, f: (h, 0, 0))],
             scratch_shapes=[
-                pltpu.VMEM((bq, 128), jnp.float32),
-                pltpu.VMEM((bq, 128), jnp.float32),
-                pltpu.VMEM((bq, head), jnp.float32),
+                pltpu.VMEM((rows, 128), jnp.float32),
+                pltpu.VMEM((rows, 128), jnp.float32),
+                pltpu.VMEM((rows, head), jnp.float32),
             ],
         ),
         out_shape=[
@@ -99,14 +112,14 @@
             jax.ShapeDtypeStruct((heads, 8, 128), jnp.float32),
         ],
         compiler_params=pltpu.CompilerParams(
-            dimension_semantics=("arbitrary",), vmem_limit_bytes=32 * 1024 * 1024
+            dimension_semantics=("arbitrary",), vmem_limit_bytes=60 * 1024 * 1024
         ),
         cost_estimate=pl.CostEstimate(
             flops=8 * rows * rows * blocks * dloc,
             bytes_accessed=4 * rows * blocks * dloc,
             transcendentals=0,
         ),
-    )(use, q, *keys, *values)
+    )(use, q, *pairs, *pairs)
 
 
 def swapped(value, axis, bit):
@@ -314,36 +327,41 @@
     yield pieces
 
 
-def project_kernel(*refs, plan, parts, head, plain):
+def project_kernel(*refs, plan, parts, head, turns, plain):
     count = max(1, len(plan))
     sources = refs[:count]
     w_ref, gain_ref, cos_ref, sin_ref = refs[count : count + 4]
-    outs = 3 if plain else 2
-    out, sum_ref = refs[count + 4 : count + 6]
-    v_ref = refs[count + 6] if plain else None
-    held, kept, lanes, mine, got, column, sems, send, recv = refs[count + 4 + outs :]
+    refs = refs[count + 4 :]
+    pairs = refs[: parts * plain]
+    refs = refs[parts * plain :]
+    outs = [None] * plain + list(refs[: turns - plain])
+    sum_ref = refs[turns - plain]
+    held, kept, lanes, mine, got, column, sems, send, recv = refs[turns - plain + 1 :]
     n, rows, depth = held.shape
     tile = kept.shape[2]
     j = pl.program_id(0)
     me = lax.axis_index("tensor")
     peers = [lax.rem(me + d, n) for d in range(1, n)]
 
-    last = (2 if plain else 1) * parts - 1
-    copies = [
-        pltpu.make_async_remote_copy(
-            src_ref=mine,
-            dst_ref=got.at[d],
-            send_sem=send.at[d],
-            recv_sem=recv.at[d],
-            device_id={"tensor": other},
-            device_id_type=MESH,
-        )
-        for d, other in enumerate(peers)
-    ]
-
-    def share():
-        pl.semaphore_wait(pltpu.get_barrier_semaphore(), n - 1)
-        for copy in copies:
+    last = (turns + plain) * parts - 1
+
+    def copies(p):
+        return [
+            pltpu.make_async_remote_copy(
+                src_ref=mine.at[p],
+                dst_ref=got.at[p, d],
+                send_sem=send.at[p, d],
+                recv_sem=recv.at[p, d],
+                device_id={"tensor": other},
+                device_id_type=MESH,
+            )
+            for d, other in enumerate(peers)
+        ]
+
+    def share(p):
+        if p == 0:
+            pl.semaphore_wait(pltpu.get_barrier_semaphore(), n - 1)
+        for copy in copies(p):
             copy.start()
 
     @pl.when(j == 0)
@@ -370,11 +388,12 @@
                     else:
                         copy.wait()
 
-    if plain:
-
-        @pl.when(j == parts)
-        def _():
-            share()
+    for p in range(turns):
+        if (p + 1) * parts <= last:
+
+            @pl.when(j == (p + 1) * parts)
+            def _():
+                share(p)
 
     total = jnp.dot(held[0], w_ref[pl.ds(0, depth), :], preferred_element_type=jnp.float32)
     for d in range(1, n):
@@ -382,7 +401,7 @@
             held[d], w_ref[pl.ds(d * depth, depth), :], preferred_element_type=jnp.float32
         )
 
-    @pl.when(j < parts)
+    @pl.when(j < turns * parts)
     def _():
         kept[j] = total
         square = total * total
@@ -390,34 +409,33 @@
         for c in range(1, tile // 128):
             part = part + square[:, c * 128 : (c + 1) * 128]
         if parts > 1:
-            part = part + jnp.where(j == 0, 0.0, lanes[...])
+            part = part + jnp.where(lax.rem(j, parts) == 0, 0.0, lanes[...])
         lanes[...] = part
 
-    @pl.when(j == parts - 1)
-    def _():
-        mine[...] = lax.dot_general(
-            jnp.ones((8, 128), jnp.float32),
-            lanes[...],
-            (((1,), (1,)), ((), ())),
-            precision=lax.Precision.HIGHEST,
-            preferred_element_type=jnp.float32,
-        )
-
-    if plain:
-
-        @pl.when(j >= parts)
-        def _():
-            v_ref[...] = total.astype(v_ref.dtype)
-
-    @pl.when(j == last)
-    def _():
-        if not plain:
-            share()
-        whole = mine[...]
-        for d, copy in enumerate(copies):
+    for p in range(turns):
+
+        @pl.when(j == (p + 1) * parts - 1)
+        def _():
+            mine[p] = lax.dot_general(
+                jnp.ones((8, 128), jnp.float32),
+                lanes[...],
+                (((1,), (1,)), ((), ())),
+                precision=lax.Precision.HIGHEST,
+                preferred_element_type=jnp.float32,
+            )
+
+    for i, pair in enumerate(pairs):
+
+        @pl.when(j == turns * parts + i)
+        def _():
+            pair[:, tile:] = total.astype(pair.dtype)
+
+    def finish(p, out):
+        whole = mine[p]
+        for d, copy in enumerate(copies(p)):
             copy.wait()
-            whole = whole + got[d]
-        sum_ref[...] = whole
+            whole = whole + got[p, d]
+        sum_ref[p] = whole
         inverse = lax.rsqrt(whole / (n * depth) + EPS)
         pick = (lax.broadcasted_iota(jnp.int32, (8, 128), 0) == 0).astype(jnp.float32)
         column[...] = lax.dot_general(
@@ -435,65 +453,89 @@
             cosine, sine, factor = cos_ref[at, :], sin_ref[at, :], column[at, :]
             for h in range(parts * tile // head):
                 from_tile, off = divmod(h * head, tile)
-                normed = kept[from_tile, at, off : off + head] * factor
-                normed = normed * gain_ref[:, h * head : (h + 1) * head]
+                normed = kept[p * parts + from_tile, at, off : off + head] * factor
+                normed = normed * gain_ref[p : p + 1, h * head : (h + 1) * head]
                 turned = normed * cosine + pltpu.roll(normed, head // 2, 1) * sine
-                out[at, h * head : (h + 1) * head] = turned.astype(out.dtype)
-
-
-def project(arrays, plan, weights, gain, cosine, sine, n, first, plain, call):
+                if out is None:
+                    pairs[from_tile][at, off : off + head] = turned.astype(jnp.bfloat16)
+                else:
+                    out[at, h * head : (h + 1) * head] = turned.astype(out.dtype)
+
+    @pl.when(j == last)
+    def _():
+        if not plain:
+            share(turns - 1)
+        for p, out in enumerate(outs):
+            finish(p, out)
+
+
+def project(arrays, plan, weights, gains, cosine, sine, n, parts, order, plain, call):
     rows, depth = arrays[0].shape[-2:]
     width, dloc = weights.shape[1:]
     head = cosine.shape[1]
-    tile = min(256, dloc)
-    parts = dloc // tile
+    tile = dloc // parts
+    turns = len(order) - plain
     dma = pltpu.SemaphoreType.DMA
 
     def weight_at(j):
-        return (first + j // parts, 0, lax.rem(j, parts))
+        part = j // parts
+        which = jnp.int32(order[-1])
+        for i, o in enumerate(order[:-1]):
+            which = jnp.where(part == i, o, which)
+        return (which, 0, lax.rem(j, parts))
 
     fixed = lambda j: (0, 0)
     result = jax.ShapeDtypeStruct((rows, dloc), jnp.bfloat16)
+    pair = jax.ShapeDtypeStruct((rows, 2 * tile), jnp.bfloat16)
     return pl.pallas_call(
-        functools.partial(project_kernel, plan=plan, parts=parts, head=head, plain=plain),
-        grid=((2 if plain else 1) * parts,),
+        functools.partial(
+            project_kernel, plan=plan, parts=parts, head=head, turns=turns, plain=plain
+        ),
+        grid=(len(order) * parts,),
         in_specs=[pl.BlockSpec(memory_space=pl.ANY)] * len(arrays)
         + [
             pl.BlockSpec((None, width, tile), weight_at),
-            pl.BlockSpec((1, dloc), fixed),
+            pl.BlockSpec((turns, dloc), fixed),
             pl.BlockSpec((rows, head), fixed),
             pl.BlockSpec((rows, head), fixed),
         ],
-        out_specs=[pl.BlockSpec((rows, dloc), fixed), pl.BlockSpec((8, rows), fixed)]
-        + [pl.BlockSpec((rows, tile), lambda j: (0, jnp.maximum(j - parts, 0)))] * plain,
-        out_shape=[result, jax.ShapeDtypeStruct((8, rows), jnp.float32)] + [result] * plain,
+        out_specs=[pl.BlockSpec((rows, 2 * tile), fixed)] * (parts * plain)
+        + [pl.BlockSpec((rows, dloc), fixed)] * (turns - plain)
+        + [pl.BlockSpec((turns, 8, rows), lambda j: (0, 0, 0))],
+        out_shape=[pair] * (parts * plain)
+        + [result] * (turns - plain)
+        + [jax.ShapeDtypeStruct((turns, 8, rows), jnp.float32)],
         scratch_shapes=[
             pltpu.VMEM((n, rows, depth), jnp.bfloat16),
-            pltpu.VMEM((parts, rows, tile), jnp.float32),
+            pltpu.VMEM((turns * parts, rows, tile), jnp.float32),
             pltpu.VMEM((rows, 128), jnp.float32),
-            pltpu.VMEM((8, rows), jnp.float32),
-            pltpu.VMEM((n - 1, 8, rows), jnp.float32),
+            pltpu.VMEM((turns, 8, rows), jnp.float32),
+            pltpu.VMEM((turns, n - 1, 8, rows), jnp.float32),
             pltpu.VMEM((rows, 128), jnp.float32),
             dma((len(arrays),)),
-            dma((n - 1,)),
-            dma((n - 1,)),
+            dma((turns, n - 1)),
+            dma((turns, n - 1)),
         ],
         compiler_params=pltpu.CompilerParams(
             dimension_semantics=("arbitrary",),
-            vmem_limit_bytes=48 * 1024 * 1024,
+            vmem_limit_bytes=60 * 1024 * 1024,
             collective_id=call,
             has_side_effects=True,
         ),
         cost_estimate=pl.CostEstimate(
-            flops=2 * (1 + plain) * rows * width * dloc,
+            flops=2 * len(order) * rows * width * dloc,
             bytes_accessed=2 * width * (rows + 3 * dloc) + 10 * rows * dloc,
             transcendentals=0,
         ),
-    )(*arrays, weights, gain, cosine, sine)
-
-
-def combine_kernel(where_ref, kept_ref, other_ref, w_ref, *refs, blocks):
-    rows_in, outs, whole = refs[:blocks], refs[blocks:-1], refs[-1]
+    )(*arrays, weights, gains, cosine, sine)
+
+
+def combine_kernel(where_ref, *refs, groups, blocks):
+    kept_refs, other_refs, refs = refs[:groups], refs[groups : 2 * groups], refs[2 * groups :]
+    w_ref, rows_in, outs = refs[0], refs[1 : 1 + blocks], refs[1 + blocks : -2]
+    whole, left = refs[-2:]
+    deep = kept_refs[0].shape[1]
+    half = groups * deep
     d = pl.program_id(0)
     share = rows_in[0].shape[0]
     dloc = w_ref.shape[1]
@@ -503,10 +545,13 @@
         for j, piece in enumerate(rows_in):
             start = pl.multiple_of((where_ref[2] ^ j) * share, share)
             whole[pl.ds(start, share), :] = piece[...]
+        for g in range(groups):
+            left[:, g * deep : (g + 1) * deep] = kept_refs[g][...]
+            left[:, half + g * deep : half + (g + 1) * deep] = other_refs[g][...]
 
     columns = pl.ds(pl.multiple_of((where_ref[0] ^ d) * dloc, dloc), dloc)
-    total = jnp.dot(kept_ref[...], w_ref[...], preferred_element_type=jnp.float32)
-    total += jnp.dot(other_ref[...], whole[:, columns], preferred_element_type=jnp.float32)
+    total = jnp.dot(left[:, :half], w_ref[...], preferred_element_type=jnp.float32)
+    total += jnp.dot(left[:, half:], whole[:, columns], preferred_element_type=jnp.float32)
     for k, out in enumerate(outs):
 
         @pl.when(d == k)
@@ -514,38 +559,40 @@
             out[...] = total.astype(out.dtype)
 
 
-def combine(where, attended, other, w_out, rows_in, n):
-    half, dloc = other.shape
-    width = w_out.shape[1]
+def combine(where, attended, others, w_out, rows_in, n):
+    half, deep = others[0].shape
+    groups = len(others)
+    dloc, width = w_out.shape
     share = rows_in[0].shape[0]
     return pl.pallas_call(
-        functools.partial(combine_kernel, blocks=len(rows_in)),
+        functools.partial(combine_kernel, groups=groups, blocks=len(rows_in)),
         grid_spec=pltpu.PrefetchScalarGridSpec(
             num_scalar_prefetch=1,
             grid=(n,),
-            in_specs=[
-                pl.BlockSpec((half, dloc), lambda d, w: (w[1], 0)),
-                pl.BlockSpec((half, dloc), lambda d, w: (0, 0)),
-                pl.BlockSpec((dloc, dloc), lambda d, w: (0, w[0] ^ d)),
-            ]
+            in_specs=[pl.BlockSpec((half, deep), lambda d, w: (w[1], 0))] * groups
+            + [pl.BlockSpec((half, deep), lambda d, w: (0, 0))] * groups
+            + [pl.BlockSpec((dloc, dloc), lambda d, w: (0, w[0] ^ d))]
             + [pl.BlockSpec((share, width), lambda d, w: (0, 0))] * len(rows_in),
             out_specs=[pl.BlockSpec((half, dloc), lambda d, w: (0, 0))] * n,
-            scratch_shapes=[pltpu.VMEM((dloc, width), w_out.dtype)],
+            scratch_shapes=[
+                pltpu.VMEM((dloc, width), w_out.dtype),
+                pltpu.VMEM((half, 2 * dloc), w_out.dtype),
+            ],
         ),
         out_shape=[jax.ShapeDtypeStruct((half, dloc), jnp.bfloat16)] * n,
         compiler_params=pltpu.CompilerParams(
-            dimension_semantics=("arbitrary",), vmem_limit_bytes=40 * 1024 * 1024
+            dimension_semantics=("arbitrary",), vmem_limit_bytes=60 * 1024 * 1024
         ),
         cost_estimate=pl.CostEstimate(
             flops=4 * half * dloc * width,
             bytes_accessed=4 * half * width + 4 * dloc * width,
             transcendentals=0,
         ),
-    )(where, attended, other, w_out, *rows_in)
+    )(where, *attended, *others, w_out, *rows_in)
 
 
 def shards(tokens, w_qkv, q_gain, k_gain, w_out):
-    seqs, tok, _ = tokens.shape
+    seqs, tok, dloc = tokens.shape
     width = w_qkv.shape[0]
     head = width // HEADS
     n = lax.axis_size("tensor")
@@ -577,32 +624,45 @@
     scale = head ** (-0.5)
     q_factor = (q_gain * (scale * LOG2E))[None]
     k_factor = k_gain[None]
+    both = jnp.concatenate([k_factor, q_factor], 0)
+    groups = 2 if (dloc // head) % 2 == 0 else 1
 
     mixed, tops, inverses = [], [], []
     for s in range(seqs):
         if s == 0:
-            arrays, plan = [whole], []
-        else:
-            weights, attended = lax.optimization_barrier((weights, attended))
-            arrays, plan = [piece[0] for piece in step], [piece[1:] for piece in step]
-        k_ready, k_sum, value = project(
-            arrays, plan, weights, k_factor, cosine, sine, n, 1, True, 1 + 2 * s
-        )
-        if s == 0:
-            *held, k_sum = lax.optimization_barrier((*step, k_sum))
+            *pairs, q_ready, square = project(
+                [whole], [], weights, both, cosine, sine, n, groups, (1, 0, 2), True, 1
+            )
+            *held, square = lax.optimization_barrier((*step, square))
             step = rest.send(tuple(held))
             while isinstance(step, tuple):
                 step = rest.send(step)
-        keys = earlier_blocks(k_ready, count, 2)
-        values = earlier_blocks(value, count, 2)
-        q_ready, q_sum = project(
-            arrays, plan, weights, q_factor, cosine, sine, n, 0, False, 2 + 2 * s
-        )
-        inverses.append(lax.rsqrt(jnp.stack([q_sum[0], k_sum[0]]) / width + EPS))
-        attended, top = flash(q_ready, keys, values, use, head)
-        tops.append(jnp.max(top, axis=(1, 2)))
-        other = swapped(block_of(attended, 1 - side, half, 0), "tensor", 2)
-        blocks = combine(where, attended, other, w_out, rows_in, n)
+            k_sum, q_sum = square[0, 0], square[1, 0]
+        else:
+            weights, *attended = lax.optimization_barrier((weights, *attended))
+            arrays, plan = [piece[0] for piece in step], [piece[1:] for piece in step]
+            *pairs, square = project(
+                arrays, plan, weights, k_factor, cosine, sine, n, groups, (1, 2), True, 2 * s
+            )
+            k_sum = square[0, 0]
+        sets = []
+        for pair in pairs:
+            sets.append(earlier_blocks(pair, count, 2))
+        if s > 0:
+            q_ready, square = project(
+                arrays, plan, weights, q_factor, cosine, sine, n, groups, (0,), False, 2 * s + 1
+            )
+            q_sum = square[0, 0]
+        inverses.append(lax.rsqrt(jnp.stack([q_sum, k_sum]) / width + EPS))
+        attended, others, parts = [], [], []
+        heads = dloc // head // groups
+        for g in range(groups):
+            made, top = flash(q_ready, sets[g], use, head, g * heads, heads)
+            attended.append(made)
+            parts.append(jnp.max(top, axis=(1, 2)))
+            others.append(swapped(block_of(made, 1 - side, half, 0), "tensor", 2))
+        tops.append(jnp.concatenate(parts))
+        blocks = combine(where, attended, others, w_out, rows_in, n)
         sums, before = {}, None
         for zd in hops + [0]:
             near = swapped(blocks[zd ^ 1], "tensor", 1)

time: 520 us -> 491 us (0.944); the launches traced: 520 us -> 483 us
  Pallas kernels: 281 us -> 255 us
  starting transfers between devices: 81.9 us -> 65.5 us
  waiting for transfers between devices: 130 us -> 138 us
    pallas_call x4 -> x3, Pallas kernels: 105 us -> 72.3 us  [project(): pl.pallas_call(functools.partial(project_kernel, plan=plan, parts=parts,...]
    ppermute x30 -> x32, starting transfers between devices: 57.9 us -> 38 us  [swapped(): return lax.ppermute(value, axis, [(i, i ^ bit) for i in range(size)])]
    ppermute x11, waiting for transfers between devices: 8.97 us -> 23.5 us  [moved(): return lax.ppermute(value, 'tensor', pairs)]
    ppermute x30 -> x32, waiting for transfers between devices: 77.9 us -> 65.7 us  [swapped(): return lax.ppermute(value, axis, [(i, i ^ bit) for i in range(size)])]
    unnamed x46 -> x68, local copies, waits for them, and re-layouts: 13 us -> 2.06 us
    pallas_call x2, Pallas kernels: 20.2 us -> 26.5 us  [combine(): pl.pallas_call(functools.partial(combine_kernel, groups=groups, blocks=le...]
    ppermute x4, waiting for transfers between devices: 43.5 us -> 48.9 us  [earlier_blocks(): lax.ppermute(block, 'seq', [(i, i + across * d) for i in range(count - ac...]
    pallas_call x2 -> x4, Pallas kernels: 59.8 us -> 60.3 us  [flash(): pl.pallas_call(functools.partial(flash_kernel, blocks=blocks, bq=bq, bk=b...]
  transfers between devices with their start and end apart: 45 -> 47, of which waited for: 15 -> 13; matrix products, arithmetic and copies ran while one was open for 1% -> 3% of each run, Pallas kernels for 32% -> 27%
where the time goes in v1:
time: 491 us; the launch traced here: 483 us
  Pallas kernels  255 us (52%)
  waiting for transfers between devices  138 us (28%)
  starting transfers between devices  65.5 us (13%)
  other arithmetic  12.7 us (3%)
  local copies, waits for them, and re-layouts  10.5 us (2%)
    pallas_call x1, Pallas kernels, gather_first(): pl.pallas_call(functools.partial(gather_kernel, line=line), in_specs=[pl....  95.3 us
    pallas_call x3, Pallas kernels, project(): pl.pallas_call(functools.partial(project_kernel, plan=plan, parts=parts,...  72.3 us
    ppermute x32, waiting for transfers between devices, swapped(): return lax.ppermute(value, axis, [(i, i ^ bit) for i in range(size)])  65.7 us
    pallas_call x4, Pallas kernels, flash(): pl.pallas_call(functools.partial(flash_kernel, blocks=blocks, bq=bq, bk=b...  60.3 us
    ppermute x4, waiting for transfers between devices, earlier_blocks(): lax.ppermute(block, 'seq', [(i, i + across * d) for i in range(count - ac...  48.9 us
    ppermute x32, starting transfers between devices, swapped(): return lax.ppermute(value, axis, [(i, i ^ bit) for i in range(size)])  38 us
    pallas_call x2, Pallas kernels, combine(): pl.pallas_call(functools.partial(combine_kernel, groups=groups, blocks=le...  26.5 us
    ppermute x11, waiting for transfers between devices, moved(): return lax.ppermute(value, 'tensor', pairs)  23.5 us
  transfers between devices with their start and end apart: 47, of which 13 were waited for; matrix products, arithmetic and copies ran while one was open for 3% of the time, Pallas kernels for 27%

profile of v1, /device:TPU:11, one launch (start us, length us, event | category | flops | bytes accessed | tf_op | source)
XLA Modules:
  0.0 483.0 jit_solution(2672478393311941635)
XLA Ops:
  0.7 95.3 %shard_map.76 = (bf16[8,1024,512]{2,1,0:T(8,128)(2,1)}, bf16[1024,512]{1,0:T(8,128)(2,1)}, bf16[1024,512]{1,0:T(8,128)(2,1)}, bf16[1024,512]{1,0:T(8,128)(2,1)}) custom-call(bf16[2,1024,512]{2,1,0:T(8,128)(2,1)} %tok_ref.1), custom_call_target="tpu_custom_call" | custom-call | flops 89999998976 | bytes 8388608 | tf_op jit(solution)/shard_map/pallas_call | solution.py:275
  96.1 1.9 fusion
  98.6 1.4 pad_maximum_fusion.1
  100.0 28.6 %shard_map.77 = (bf16[1024,512]{1,0:T(8,128)(2,1)}, bf16[1024,512]{1,0:T(8,128)(2,1)}, bf16[1024,512]{1,0:T(8,128)(2,1)}, f32[2,8,1024]{2,1,0:T(8,128)}) custom-call(bf16[8,1024,512]{2,1,0:T(8,128)(2,1)} %get-tuple-element.50.refs_0_, bf16[3,4096,512]{2,1,0:T(8,128)(2,1)} %bitcast.12, f32[2,512]{1,0:T(2,128)} %pad_maximum_fusion.4.refs_2_, ...), custom_call_target="tpu_custom_call" | custom-call | flops 12884901888 | bytes 26214400 | tf_op jit(solution)/shard_map/pallas_call | solution.py:490
  129.9 2.2 collective-permute-start.3
  133.4 3.4 collective-permute-start.20
  136.8 16.6 %collective-permute-done.4.refs_2_.refs_6_ = bf16[1024,512]{1,0:T(8,128)(2,1)} collective-permute-done((bf16[1024,512]{1,0:T(8,128)(2,1)}, bf16[1024,512]{1,0:T(8,128)(2,1)}, u32[]{:S(2)}, u32[]{:S(2)}) %collective-permute-start.4) | collective-permute-done | bytes 1048608 | tf_op jit(solution)/shard_map/ppermute | solution.py:132
  153.4 1.9 collective-permute-start.21
  155.3 2.3 collective-permute-start.22
  157.6 18.2 %collective-permute-done.1.refs_2_.refs_6_ = bf16[1024,512]{1,0:T(8,128)(2,1)} collective-permute-done((bf16[1024,512]{1,0:T(8,128)(2,1)}, bf16[1024,512]{1,0:T(8,128)(2,1)}, u32[]{:S(2)}, u32[]{:S(2)}) %collective-permute-start.1) | collective-permute-done | bytes 1048608 | tf_op jit(solution)/shard_map/ppermute | solution.py:132
  175.9 1.9 collective-permute-start.23
  177.8 1.9 collective-permute-start.19
  179.7 3.4 collective-permute-start.5
  183.1 2.4 collective-permute-start.2
  186.2 13.4 %collective-permute-done.23.refs_7_ = bf16[1024,512]{1,0:T(8,128)(2,1)} collective-permute-done((bf16[1024,512]{1,0:T(8,128)(2,1)S(1)}, bf16[1024,512]{1,0:T(8,128)(2,1)}, u32[]{:S(2)}, u32[]{:S(2)}) %collective-permute-start.23) | collective-permute-done | bytes 1048608 | tf_op jit(solution)/shard_map/ppermute | solution.py:296
  199.6 2.2 collective-permute-start.27
  202.5 2.3 constant_dynamic-slice_fusion.2
  205.6 3.7 collective-permute-start.25
  209.3 1.6 collective-permute-start.28
  210.9 10.0 %collective-permute-done.27.refs_11_ = bf16[1024,512]{1,0:T(8,128)(2,1)S(1)} collective-permute-done((bf16[1024,512]{1,0:T(8,128)(2,1)}, bf16[1024,512]{1,0:T(8,128)(2,1)S(1)}, u32[]{:S(2)}, u32[]{:S(2)}) %collective-permute-start.27) | collective-permute-done | bytes 1048608 | tf_op jit(solution)/shard_map/ppermute | solution.py:296
  221.0 2.1 collective-permute-start.29
  223.0 15.0 %shard_map.79 = (bf16[1024,256]{1,0:T(8,128)(2,1)}, f32[2,8,128]{2,1,0:T(8,128)}) custom-call(s32[4]{0:T(128)} %pad_add_fusion.1.use_ref, bf16[1024,512]{1,0:T(8,128)(2,1)} %get-tuple-element.51.q_ref, bf16[1024,512]{1,0:T(8,128)(2,1)} %get-tuple-element.54.refs_0_.refs_4_, bf16[1024,512]{1,0:T(8,128)(2,1)} %copy-done.27, ...), custom_call_target="tpu_custom_call" | custom-call | flops 8589934592 | bytes 4194304 | tf_op jit(solution)/shard_map/pallas_call | solution.py:97
  238.1 15.0 %shard_map.78 = (bf16[1024,256]{1,0:T(8,128)(2,1)}, f32[2,8,128]{2,1,0:T(8,128)}) custom-call(s32[4]{0:T(128)} %pad_add_fusion.1.use_ref, bf16[1024,512]{1,0:T(8,128)(2,1)} %get-tuple-element.51.q_ref, bf16[1024,512]{1,0:T(8,128)(2,1)} %get-tuple-element.52.refs_0_.refs_4_, bf16[1024,512]{1,0:T(8,128)(2,1)} %copy-done.28, ...), custom_call_target="tpu_custom_call" | custom-call | flops 8589934592 | bytes 4194304 | tf_op jit(solution)/shard_map/pallas_call | solution.py:97
  253.2 2.5 collective-permute-start.9
  255.7 20.7 %shard_map.82 = (bf16[1024,512]{1,0:T(8,128)(2,1)}, bf16[1024,512]{1,0:T(8,128)(2,1)}, f32[1,8,1024]{2,1,0:T(8,128)}) custom-call(bf16[1024,512]{1,0:T(8,128)(2,1)} %get-tuple-element.67.refs_0_, bf16[1024,512]{1,0:T(8,128)(2,1)} %collective-permute-done.19.refs_1_, bf16[1024,512]{1,0:T(8,128)(2,1)} %get-tuple-element.71.refs_2_, ...), custom_call_target="tpu_custom_call" | custom-call | flops 8589934592 | bytes 26214400 | tf_op jit(solution)/shard_map/pallas_call | solution.py:490
  277.7 1.8 collective-permute-start.11
  281.2 3.9 collective-permute-start.7
  287.4 14.1 %collective-permute-done.34.refs_2_.refs_6_ = bf16[1024,512]{1,0:T(8,128)(2,1)S(1)} collective-permute-done((bf16[1024,512]{1,0:T(8,128)(2,1)}, bf16[1024,512]{1,0:T(8,128)(2,1)S(1)}, u32[]{:S(2)}, u32[]{:S(2)}) %collective-permute-start.34) | collective-permute-done | bytes 1048608 | tf_op jit(solution)/shard_map/ppermute | solution.py:132
  301.5 4.7 collective-permute-start.35
  308.2 2.4 collective-permute-start.6
  310.5 23.1 %shard_map.81 = (bf16[1024,512]{1,0:T(8,128)(2,1)}, f32[1,8,1024]{2,1,0:T(8,128)}) custom-call(bf16[1024,512]{1,0:T(8,128)(2,1)} %get-tuple-element.67.refs_0_, bf16[1024,512]{1,0:T(8,128)(2,1)} %collective-permute-done.19.refs_1_, bf16[1024,512]{1,0:T(8,128)(2,1)} %get-tuple-element.71.refs_2_, bf16[1024,512]{1,0:T(8,128)(2,1)} %get-tuple-element.72.refs_3_, ...), custom_call_target="tpu_custom_call" | custom-call | flops 4294967296 | bytes 26214400 | tf_op jit(solution)/shard_map/pallas_call | solution.py:490
  336.2 13.3 %shard_map.80 = (bf16[512,512]{1,0:T(8,128)(2,1)}, bf16[512,512]{1,0:T(8,128)(2,1)}, bf16[512,512]{1,0:T(8,128)(2,1)}, bf16[512,512]{1,0:T(8,128)(2,1)}, bf16[51...) custom-call(s32[3]{0:T(128)} %pad_add_fusion.where_ref, ...), custom_call_target="tpu_custom_call" | custom-call | flops 4294967296 | bytes 16777216 | tf_op jit(solution)/shard_map/pallas_call | solution.py:567
  353.3 15.0 %shard_map.84 = (bf16[1024,256]{1,0:T(8,128)(2,1)}, f32[2,8,128]{2,1,0:T(8,128)}) custom-call(s32[4]{0:T(128)} %pad_add_fusion.1.use_ref, bf16[1024,512]{1,0:T(8,128)(2,1)} %get-tuple-element.74.q_ref, bf16[1024,512]{1,0:T(8,128)(2,1)} %get-tuple-element.77.refs_0_.refs_4_, bf16[1024,512]{1,0:T(8,128)(2,1)} %collective-permute-done.33.refs_1_.refs_5_, ...), custom_call_target="tpu_custom_call" | custom-call | flops 8589934592 | bytes 4194304 | tf_op jit(solution)/shard_map/pallas_call | solution.py:97
  369.9 15.2 %shard_map.83 = (bf16[1024,256]{1,0:T(8,128)(2,1)}, f32[2,8,128]{2,1,0:T(8,128)}) custom-call(s32[4]{0:T(128)} %pad_add_fusion.1.use_ref, bf16[1024,512]{1,0:T(8,128)(2,1)} %get-tuple-element.74.q_ref, bf16[1024,512]{1,0:T(8,128)(2,1)} %get-tuple-element.75.refs_0_.refs_4_, bf16[1024,512]{1,0:T(8,128)(2,1)} %collective-permute-done.30.refs_1_.refs_5_, ...), custom_call_target="tpu_custom_call" | custom-call | flops 8589934592 | bytes 4194304 | tf_op jit(solution)/shard_map/pallas_call | solution.py:97
  386.1 1.5 collective-permute-start.36
  387.9 12.5 %collective-permute-done.36.refs_2_ = bf16[512,256]{1,0:T(8,128)(2,1)S(1)} collective-permute-done((bf16[512,256]{1,0:T(8,128)(2,1)S(1)}, bf16[512,256]{1,0:T(8,128)(2,1)S(1)}, u32[]{:S(2)}, u32[]{:S(2)}) %collective-permute-start.36) | collective-permute-done | bytes 262176 | tf_op jit(solution)/shard_map/ppermute | solution.py:127
  401.2 13.3 %shard_map.85 = (bf16[512,512]{1,0:T(8,128)(2,1)}, bf16[512,512]{1,0:T(8,128)(2,1)}, bf16[512,512]{1,0:T(8,128)(2,1)}, bf16[512,512]{1,0:T(8,128)(2,1)}, bf16[51...) custom-call(s32[3]{0:T(128)} %pad_add_fusion.where_ref, ...), custom_call_target="tpu_custom_call" | custom-call | flops 4294967296 | bytes 16777216 | tf_op jit(solution)/shard_map/pallas_call | solution.py:567
  414.7 3.4 collective-permute-start.16
  418.8 9.8 %collective-permute-done.41 = bf16[512,512]{1,0:T(8,128)(2,1)S(1)} collective-permute-done((bf16[512,512]{1,0:T(8,128)(2,1)}, bf16[512,512]{1,0:T(8,128)(2,1)S(1)}, u32[]{:S(2)}, u32[]{:S(2)}) %collective-permute-start.41) | collective-permute-done | bytes 524320 | tf_op jit(solution)/shard_map/ppermute | solution.py:127
  428.8 11.2 %collective-permute-done.40 = bf16[512,512]{1,0:T(8,128)(2,1)S(1)} collective-permute-done((bf16[512,512]{1,0:T(8,128)(2,1)}, bf16[512,512]{1,0:T(8,128)(2,1)S(1)}, u32[]{:S(2)}, u32[]{:S(2)}) %collective-permute-start.40) | collective-permute-done | bytes 524320 | tf_op jit(solution)/shard_map/ppermute | solution.py:127
  440.2 5.7 %collective-permute-done.39 = bf16[512,512]{1,0:T(8,128)(2,1)S(1)} collective-permute-done((bf16[512,512]{1,0:T(8,128)(2,1)S(1)}, bf16[512,512]{1,0:T(8,128)(2,1)S(1)}, u32[]{:S(2)}, u32[]{:S(2)}) %collective-permute-start.39) | collective-permute-done | bytes 524320 | tf_op jit(solution)/shard_map/ppermute | solution.py:127
  446.1 4.3 collective-permute-start.43
  450.5 1.5 select_convert_fusion.3
  453.5 2.8 collective-permute-done.46
  456.9 13.8 %collective-permute-done.44 = bf16[512,512]{1,0:T(8,128)(2,1)} collective-permute-done((bf16[512,512]{1,0:T(8,128)(2,1)S(1)}, bf16[512,512]{1,0:T(8,128)(2,1)}, u32[]{:S(2)}, u32[]{:S(2)}) %collective-permute-start.44) | collective-permute-done | bytes 524320 | tf_op jit(solution)/shard_map/ppermute | solution.py:127
  470.7 8.7 %collective-permute-done.43 = bf16[512,512]{1,0:T(8,128)(2,1)} collective-permute-done((bf16[512,512]{1,0:T(8,128)(2,1)S(1)}, bf16[512,512]{1,0:T(8,128)(2,1)}, u32[]{:S(2)}, u32[]{:S(2)}) %collective-permute-start.43) | collective-permute-done | bytes 524320 | tf_op jit(solution)/shard_map/ppermute | solution.py:127
  479.3 1.9 select_convert_fusion.1
  481.3 1.5 pad_maximum_fusion
  (161 shorter events, 26.2 us)
Async XLA Ops:
  0.7 97.3 %copy-start.24 = (f32[512]{0:T(512)S(1)}, f32[512]{0:T(512)}, u32[]{:S(2)}) copy-start(f32[512]{0:T(512)} %param.8) | copy-start | bytes 6148
  128.6 24.8 %collective-permute-start.4 = (bf16[1024,512]{1,0:T(8,128)(2,1)}, bf16[1024,512]{1,0:T(8,128)(2,1)}, u32[]{:S(2)}, u32[]{:S(2)}) collective-permute-start(bf16[1024,512]{1,0:T(8,128)(2,1)} %get-tuple-element.54.refs_0_.refs_4_), channel_id=1, source_target_pairs={{0,16},{8,24},{1,17},{9,25},{2,18},{10,26},{3,19},{11,27},{4,20},{... | collective-permute-start | bytes 3145736 | tf_op jit(solution)/shard_map/ppermute | solution.py:132
  129.9 25.4 %collective-permute-start.3 = (bf16[1024,512]{1,0:T(8,128)(2,1)}, bf16[1024,512]{1,0:T(8,128)(2,1)S(1)}, u32[]{:S(2)}, u32[]{:S(2)}) collective-permute-start(bf16[1024,512]{1,0:T(8,128)(2,1)} %get-tuple-element.54.refs_0_.refs_4_), channel_id=1, source_target_pairs={{0,8},{8,0},{16,24},{24,16},{1,9},{9,1},{17,25},{25,17},{2,10},{10... | collective-permute-start | bytes 3145736 | tf_op jit(solution)/shard_map/ppermute | solution.py:127
  132.0 43.8 %collective-permute-start.1 = (bf16[1024,512]{1,0:T(8,128)(2,1)}, bf16[1024,512]{1,0:T(8,128)(2,1)}, u32[]{:S(2)}, u32[]{:S(2)}) collective-permute-start(bf16[1024,512]{1,0:T(8,128)(2,1)} %get-tuple-element.52.refs_0_.refs_4_), channel_id=1, source_target_pairs={{0,16},{8,24},{1,17},{9,25},{2,18},{10,26},{3,19},{11,27},{4,20},{... | collective-permute-start | bytes 3145736 | tf_op jit(solution)/shard_map/ppermute | solution.py:132
  133.3 44.5 %collective-permute-start = (bf16[1024,512]{1,0:T(8,128)(2,1)}, bf16[1024,512]{1,0:T(8,128)(2,1)S(1)}, u32[]{:S(2)}, u32[]{:S(2)}) collective-permute-start(bf16[1024,512]{1,0:T(8,128)(2,1)} %get-tuple-element.52.refs_0_.refs_4_), channel_id=1, source_target_pairs={{0,8},{8,0},{16,24},{24,16},{1,9},{9,1},{17,25},{25,17},{2,10},{10... | collective-permute-start | bytes 3145736 | tf_op jit(solution)/shard_map/ppermute | solution.py:127
  133.4 46.3 %collective-permute-start.20 = (bf16[1024,512]{1,0:T(8,128)(2,1)S(1)}, bf16[1024,512]{1,0:T(8,128)(2,1)S(1)}, u32[]{:S(2)}, u32[]{:S(2)}) collective-permute-start(bf16[1024,512]{1,0:T(8,128)(2,1)S(1)} %copy-done.1), channel_id=1, source_target_pairs={{2,3},{3,2},{4,5},{5,4},{6,7},{7,6},{10,11},{11,10},{12,13},{13,12... | collective-permute-start | bytes 3145736 | tf_op jit(solution)/shard_map/ppermute | solution.py:296
  153.4 29.7 %collective-permute-start.21 = (bf16[1024,512]{1,0:T(8,128)(2,1)S(1)}, bf16[1024,512]{1,0:T(8,128)(2,1)S(1)}, u32[]{:S(2)}, u32[]{:S(2)}) collective-permute-start(bf16[1024,512]{1,0:T(8,128)(2,1)S(1)} %copy-done.2), channel_id=1, source_target_pairs={{0,1},{1,0},{2,3},{3,2},{4,5},{5,4},{8,9},{9,8},{10,11},{11,10},{1... | collective-permute-start | bytes 3145736 | tf_op jit(solution)/shard_map/ppermute | solution.py:296
  155.3 30.2 %collective-permute-start.22 = (bf16[1024,512]{1,0:T(8,128)(2,1)S(1)}, bf16[1024,512]{1,0:T(8,128)(2,1)}, u32[]{:S(2)}, u32[]{:S(2)}) collective-permute-start(bf16[1024,512]{1,0:T(8,128)(2,1)S(1)} %copy-done.1), channel_id=1, source_target_pairs={{2,4},{3,5},{4,6},{5,7},{10,12},{11,13},{12,14},{13,15},{18,20},{1... | collective-permute-start | bytes 3145736 | tf_op jit(solution)/shard_map/ppermute | solution.py:296
  175.9 23.7 %collective-permute-start.23 = (bf16[1024,512]{1,0:T(8,128)(2,1)S(1)}, bf16[1024,512]{1,0:T(8,128)(2,1)}, u32[]{:S(2)}, u32[]{:S(2)}) collective-permute-start(bf16[1024,512]{1,0:T(8,128)(2,1)S(1)} %copy-done.2), channel_id=1, source_target_pairs={{2,0},{3,1},{4,2},{5,3},{10,8},{11,9},{12,10},{13,11},{18,16},{19,... | collective-permute-start | bytes 3145736 | tf_op jit(solution)/shard_map/ppermute | solution.py:296
  177.8 27.0 %collective-permute-start.19 = (bf16[1024,512]{1,0:T(8,128)(2,1)S(1)}, bf16[1024,512]{1,0:T(8,128)(2,1)}, u32[]{:S(2)}, u32[]{:S(2)}) collective-permute-start(bf16[1024,512]{1,0:T(8,128)(2,1)S(1)} %copy-done), channel_id=1, source_target_pairs={{0,1},{1,0},{2,3},{3,2},{4,5},{5,4},{6,7},{7,6},{8,9},{9,8},{10,11... | collective-permute-start | bytes 3145736 | tf_op jit(solution)/shard_map/ppermute | solution.py:296
  179.7 25.1 %collective-permute-start.5 = (bf16[1024,512]{1,0:T(8,128)(2,1)}, bf16[1024,512]{1,0:T(8,128)(2,1)}, u32[]{:S(2)}, u32[]{:S(2)}) collective-permute-start(bf16[1024,512]{1,0:T(8,128)(2,1)} %collective-permute-done.4.refs_2_.refs_6_), channel_id=1, source_target_pairs={{0,8},{8,0},{16,24},{24,16},{1,9},{9,1},{17,25},{25,17},{2,10},{10... | collective-permute-start | bytes 3145736 | tf_op jit(solution)/shard_map/ppermute | solution.py:127
  183.1 22.5 %collective-permute-start.2 = (bf16[1024,512]{1,0:T(8,128)(2,1)}, bf16[1024,512]{1,0:T(8,128)(2,1)}, u32[]{:S(2)}, u32[]{:S(2)}) collective-permute-start(bf16[1024,512]{1,0:T(8,128)(2,1)} %collective-permute-done.1.refs_2_.refs_6_), channel_id=1, source_target_pairs={{0,8},{8,0},{16,24},{24,16},{1,9},{9,1},{17,25},{25,17},{2,10},{10... | collective-permute-start | bytes 3145736 | tf_op jit(solution)/shard_map/ppermute | solution.py:127
  185.5 23.8 %collective-permute-start.26 = (bf16[1024,512]{1,0:T(8,128)(2,1)}, bf16[1024,512]{1,0:T(8,128)(2,1)S(1)}, u32[]{:S(2)}, u32[]{:S(2)}) collective-permute-start(bf16[1024,512]{1,0:T(8,128)(2,1)} %collective-permute-done.22.refs_6_), channel_id=1, source_target_pairs={{4,6},{5,7},{12,14},{13,15},{20,22},{21,23},{28,30},{29,31}} | collective-permute-start | bytes 3145736 | tf_op jit(solution)/shard_map/ppermute | solution.py:296
  199.6 21.3 %collective-permute-start.27 = (bf16[1024,512]{1,0:T(8,128)(2,1)}, bf16[1024,512]{1,0:T(8,128)(2,1)S(1)}, u32[]{:S(2)}, u32[]{:S(2)}) collective-permute-start(bf16[1024,512]{1,0:T(8,128)(2,1)} %collective-permute-done.23.refs_7_), channel_id=1, source_target_pairs={{2,0},{3,1},{10,8},{11,9},{18,16},{19,17},{26,24},{27,25}} | collective-permute-start | bytes 3145736 | tf_op jit(solution)/shard_map/ppermute | solution.py:296
  204.8 48.3 %collective-permute-start.8 = (bf16[128,4096]{1,0:T(8,128)(2,1)}, bf16[128,4096]{1,0:T(8,128)(2,1)}, u32[]{:S(2)}, u32[]{:S(2)}) collective-permute-start(bf16[128,4096]{1,0:T(8,128)(2,1)} %constant_dynamic-slice_fusion.2), channel_id=1, source_target_pairs={{0,2},{1,3},{2,0},{3,1},{4,6},{5,7},{6,4},{7,5},{8,10},{9,11},{10,... | collective-permute-start | bytes 3145736 | tf_op jit(solution)/shard_map/ppermute | solution.py:127
  204.8 48.4 %collective-permute-start.24 = (bf16[1024,512]{1,0:T(8,128)(2,1)}, bf16[1024,512]{1,0:T(8,128)(2,1)S(1)}, u32[]{:S(2)}, u32[]{:S(2)}) collective-permute-start(bf16[1024,512]{1,0:T(8,128)(2,1)} %collective-permute-done.22.refs_6_), channel_id=1, source_target_pairs={{4,5},{5,4},{6,7},{7,6},{12,13},{13,12},{14,15},{15,14},{20,21},{2... | collective-permute-start | bytes 3145736 | tf_op jit(solution)/shard_map/ppermute | solution.py:296
  205.6 50.1 %collective-permute-start.25 = (bf16[1024,512]{1,0:T(8,128)(2,1)}, bf16[1024,512]{1,0:T(8,128)(2,1)}, u32[]{:S(2)}, u32[]{:S(2)}) collective-permute-start(bf16[1024,512]{1,0:T(8,128)(2,1)} %collective-permute-done.23.refs_7_), channel_id=1, source_target_pairs={{0,1},{1,0},{2,3},{3,2},{8,9},{9,8},{10,11},{11,10},{16,17},{17,16... | collective-permute-start | bytes 3145736 | tf_op jit(solution)/shard_map/ppermute | solution.py:296
  209.3 46.4 %collective-permute-start.28 = (bf16[1024,512]{1,0:T(8,128)(2,1)S(1)}, bf16[1024,512]{1,0:T(8,128)(2,1)}, u32[]{:S(2)}, u32[]{:S(2)}) collective-permute-start(bf16[1024,512]{1,0:T(8,128)(2,1)S(1)} %collective-permute-done.26.refs_10_), channel_id=1, source_target_pairs={{6,7},{7,6},{14,15},{15,14},{22,23},{23,22},{30,31},{31,30}} | collective-permute-start | bytes 3145736 | tf_op jit(solution)/shard_map/ppermute | solution.py:296
  221.0 34.7 %collective-permute-start.29 = (bf16[1024,512]{1,0:T(8,128)(2,1)S(1)}, bf16[1024,512]{1,0:T(8,128)(2,1)}, u32[]{:S(2)}, u32[]{:S(2)}) collective-permute-start(bf16[1024,512]{1,0:T(8,128)(2,1)S(1)} %collective-permute-done.27.refs_11_), channel_id=1, source_target_pairs={{0,1},{1,0},{8,9},{9,8},{16,17},{17,16},{24,25},{25,24}} | collective-permute-start | bytes 3145736 | tf_op jit(solution)/shard_map/ppermute | solution.py:296
  253.1 24.6 %collective-permute-start.10 = (bf16[128,4096]{1,0:T(8,128)(2,1)}, bf16[128,4096]{1,0:T(8,128)(2,1)}, u32[]{:S(2)}, u32[]{:S(2)}) collective-permute-start(bf16[128,4096]{1,0:T(8,128)(2,1)} %collective-permute-done.8.refs_5_), channel_id=1, source_target_pairs={{0,16},{8,24},{16,0},{24,8},{1,17},{9,25},{17,1},{25,9},{2,18},{10... | collective-permute-start | bytes 3145736 | tf_op jit(solution)/shard_map/ppermute | solution.py:127
  253.2 33.8 %collective-permute-start.9 = (bf16[128,4096]{1,0:T(8,128)(2,1)}, bf16[128,4096]{1,0:T(8,128)(2,1)}, u32[]{:S(2)}, u32[]{:S(2)}) collective-permute-start(bf16[128,4096]{1,0:T(8,128)(2,1)} %collective-permute-done.8.refs_5_), channel_id=1, source_target_pairs={{0,8},{8,0},{16,24},{24,16},{1,9},{9,1},{17,25},{25,17},{2,10},{10... | collective-permute-start | bytes 3145736 | tf_op jit(solution)/shard_map/ppermute | solution.py:127
  276.4 25.1 %collective-permute-start.34 = (bf16[1024,512]{1,0:T(8,128)(2,1)}, bf16[1024,512]{1,0:T(8,128)(2,1)S(1)}, u32[]{:S(2)}, u32[]{:S(2)}) collective-permute-start(bf16[1024,512]{1,0:T(8,128)(2,1)} %get-tuple-element.77.refs_0_.refs_4_), channel_id=1, source_target_pairs={{0,16},{8,24},{1,17},{9,25},{2,18},{10,26},{3,19},{11,27},{4,20},{... | collective-permute-start | bytes 3145736 | tf_op jit(solution)/shard_map/ppermute | solution.py:132
  277.7 57.3 %collective-permute-start.11 = (bf16[128,4096]{1,0:T(8,128)(2,1)}, bf16[128,4096]{1,0:T(8,128)(2,1)S(1)}, u32[]{:S(2)}, u32[]{:S(2)}) collective-permute-start(bf16[128,4096]{1,0:T(8,128)(2,1)} %collective-permute-done.10.refs_7_), channel_id=1, source_target_pairs={{0,8},{8,0},{16,24},{24,16},{1,9},{9,1},{17,25},{25,17},{2,10},{10... | collective-permute-start | bytes 3145736 | tf_op jit(solution)/shard_map/ppermute | solution.py:127
  281.2 26.9 %collective-permute-start.7 = (bf16[512,256]{1,0:T(8,128)(2,1)S(1)}, bf16[512,256]{1,0:T(8,128)(2,1)S(1)}, u32[]{:S(2)}, u32[]{:S(2)}) collective-permute-start(bf16[512,256]{1,0:T(8,128)(2,1)S(1)} %constant_dynamic-slice_fusion.3), channel_id=1, source_target_pairs={{0,2},{1,3},{2,0},{3,1},{4,6},{5,7},{6,4},{7,5},{8,10},{9,11},{10,... | collective-permute-start | bytes 786440 | tf_op jit(solution)/shard_map/ppermute | solution.py:127
  285.1 65.3 %collective-permute-start.31 = (bf16[1024,512]{1,0:T(8,128)(2,1)}, bf16[1024,512]{1,0:T(8,128)(2,1)}, u32[]{:S(2)}, u32[]{:S(2)}) collective-permute-start(bf16[1024,512]{1,0:T(8,128)(2,1)} %get-tuple-element.75.refs_0_.refs_4_), channel_id=1, source_target_pairs={{0,16},{8,24},{1,17},{9,25},{2,18},{10,26},{3,19},{11,27},{4,20},{... | collective-permute-start | bytes 3145736 | tf_op jit(solution)/shard_map/ppermute | solution.py:132
  287.1 64.7 %collective-permute-start.33 = (bf16[1024,512]{1,0:T(8,128)(2,1)}, bf16[1024,512]{1,0:T(8,128)(2,1)}, u32[]{:S(2)}, u32[]{:S(2)}) collective-permute-start(bf16[1024,512]{1,0:T(8,128)(2,1)} %get-tuple-element.77.refs_0_.refs_4_), channel_id=1, source_target_pairs={{0,8},{8,0},{16,24},{24,16},{1,9},{9,1},{17,25},{25,17},{2,10},{10... | collective-permute-start | bytes 3145736 | tf_op jit(solution)/shard_map/ppermute | solution.py:127
  301.5 50.9 %collective-permute-start.35 = (bf16[1024,512]{1,0:T(8,128)(2,1)S(1)}, bf16[1024,512]{1,0:T(8,128)(2,1)}, u32[]{:S(2)}, u32[]{:S(2)}) collective-permute-start(bf16[1024,512]{1,0:T(8,128)(2,1)S(1)} %collective-permute-done.34.refs_2_.refs_6_), channel_id=1, source_target_pairs={{0,8},{8,0},{16,24},{24,16},{1,9},{9,1},{17,25},{25,17},{2,10},{10... | collective-permute-start | bytes 3145736 | tf_op jit(solution)/shard_map/ppermute | solution.py:127
  308.2 26.3 %collective-permute-start.6 = (bf16[512,256]{1,0:T(8,128)(2,1)S(1)}, bf16[512,256]{1,0:T(8,128)(2,1)S(1)}, u32[]{:S(2)}, u32[]{:S(2)}) collective-permute-start(bf16[512,256]{1,0:T(8,128)(2,1)S(1)} %constant_dynamic-slice_fusion.4), channel_id=1, source_target_pairs={{0,2},{1,3},{2,0},{3,1},{4,6},{5,7},{6,4},{7,5},{8,10},{9,11},{10,... | collective-permute-start | bytes 786440 | tf_op jit(solution)/shard_map/ppermute | solution.py:127
  334.5 34.8 %collective-permute-start.30 = (bf16[1024,512]{1,0:T(8,128)(2,1)}, bf16[1024,512]{1,0:T(8,128)(2,1)}, u32[]{:S(2)}, u32[]{:S(2)}) collective-permute-start(bf16[1024,512]{1,0:T(8,128)(2,1)} %get-tuple-element.75.refs_0_.refs_4_), channel_id=1, source_target_pairs={{0,8},{8,0},{16,24},{24,16},{1,9},{9,1},{17,25},{25,17},{2,10},{10... | collective-permute-start | bytes 3145736 | tf_op jit(solution)/shard_map/ppermute | solution.py:127
  349.4 36.7 %collective-permute-start.15 = (bf16[512,512]{1,0:T(8,128)(2,1)}, bf16[512,512]{1,0:T(8,128)(2,1)S(1)}, u32[]{:S(2)}, u32[]{:S(2)}) collective-permute-start(bf16[512,512]{1,0:T(8,128)(2,1)} %get-tuple-element.63), channel_id=1, source_target_pairs={{0,1},{1,0},{2,3},{3,2},{4,5},{5,4},{6,7},{7,6},{8,9},{9,8},{10,11... | collective-permute-start | bytes 1572872 | tf_op jit(solution)/shard_map/ppermute | solution.py:127
  350.4 19.5 %collective-permute-start.32 = (bf16[1024,512]{1,0:T(8,128)(2,1)}, bf16[1024,512]{1,0:T(8,128)(2,1)}, u32[]{:S(2)}, u32[]{:S(2)}) collective-permute-start(bf16[1024,512]{1,0:T(8,128)(2,1)} %collective-permute-done.31.refs_2_.refs_6_), channel_id=1, source_target_pairs={{0,8},{8,0},{16,24},{24,16},{1,9},{9,1},{17,25},{25,17},{2,10},{10... | collective-permute-start | bytes 3145736 | tf_op jit(solution)/shard_map/ppermute | solution.py:127
  351.8 36.1 %collective-permute-start.14 = (bf16[512,512]{1,0:T(8,128)(2,1)}, bf16[512,512]{1,0:T(8,128)(2,1)S(1)}, u32[]{:S(2)}, u32[]{:S(2)}) collective-permute-start(bf16[512,512]{1,0:T(8,128)(2,1)} %get-tuple-element.61), channel_id=1, source_target_pairs={{0,1},{1,0},{2,3},{3,2},{4,5},{5,4},{6,7},{7,6},{8,9},{9,8},{10,11... | collective-permute-start | bytes 1572872 | tf_op jit(solution)/shard_map/ppermute | solution.py:127
  352.4 65.7 %collective-permute-start.13 = (bf16[512,512]{1,0:T(8,128)(2,1)}, bf16[512,512]{1,0:T(8,128)(2,1)S(1)}, u32[]{:S(2)}, u32[]{:S(2)}) collective-permute-start(bf16[512,512]{1,0:T(8,128)(2,1)} %get-tuple-element.59), channel_id=1, source_target_pairs={{0,1},{1,0},{2,3},{3,2},{4,5},{5,4},{6,7},{7,6},{8,9},{9,8},{10,11... | collective-permute-start | bytes 1572872 | tf_op jit(solution)/shard_map/ppermute | solution.py:127
  369.3 49.5 %collective-permute-start.12 = (bf16[512,512]{1,0:T(8,128)(2,1)}, bf16[512,512]{1,0:T(8,128)(2,1)S(1)}, u32[]{:S(2)}, u32[]{:S(2)}) collective-permute-start(bf16[512,512]{1,0:T(8,128)(2,1)} %get-tuple-element.57), channel_id=1, source_target_pairs={{0,1},{1,0},{2,3},{3,2},{4,5},{5,4},{6,7},{7,6},{8,9},{9,8},{10,11... | collective-permute-start | bytes 1572872 | tf_op jit(solution)/shard_map/ppermute | solution.py:127
  369.9 18.0 %collective-permute-start.37 = (bf16[512,256]{1,0:T(8,128)(2,1)S(1)}, bf16[512,256]{1,0:T(8,128)(2,1)S(1)}, u32[]{:S(2)}, u32[]{:S(2)}) collective-permute-start(bf16[512,256]{1,0:T(8,128)(2,1)S(1)} %constant_dynamic-slice_fusion), channel_id=1, source_target_pairs={{0,2},{1,3},{2,0},{3,1},{4,6},{5,7},{6,4},{7,5},{8,10},{9,11},{10,... | collective-permute-start | bytes 786440 | tf_op jit(solution)/shard_map/ppermute | solution.py:127
  386.1 14.3 %collective-permute-start.36 = (bf16[512,256]{1,0:T(8,128)(2,1)S(1)}, bf16[512,256]{1,0:T(8,128)(2,1)S(1)}, u32[]{:S(2)}, u32[]{:S(2)}) collective-permute-start(bf16[512,256]{1,0:T(8,128)(2,1)S(1)} %constant_dynamic-slice_fusion.1), channel_id=1, source_target_pairs={{0,2},{1,3},{2,0},{3,1},{4,6},{5,7},{6,4},{7,5},{8,10},{9,11},{10,... | collective-permute-start | bytes 786440 | tf_op jit(solution)/shard_map/ppermute | solution.py:127
  387.8 62.6 %collective-permute-start.17 = (bf16[512,512]{1,0:T(8,128)(2,1)S(1)}, bf16[512,512]{1,0:T(8,128)(2,1)}, u32[]{:S(2)}, u32[]{:S(2)}) collective-permute-start(bf16[512,512]{1,0:T(8,128)(2,1)S(1)} %add_convert_fusion.5), channel_id=1, source_target_pairs={{0,6},{1,7},{2,4},{3,5},{4,2},{5,3},{6,0},{7,1},{8,14},{9,15},{10,... | collective-permute-start | bytes 1572872 | tf_op jit(solution)/shard_map/ppermute | solution.py:127
  414.5 14.2 %collective-permute-start.41 = (bf16[512,512]{1,0:T(8,128)(2,1)}, bf16[512,512]{1,0:T(8,128)(2,1)S(1)}, u32[]{:S(2)}, u32[]{:S(2)}) collective-permute-start(bf16[512,512]{1,0:T(8,128)(2,1)} %get-tuple-element.86), channel_id=1, source_target_pairs={{0,1},{1,0},{2,3},{3,2},{4,5},{5,4},{6,7},{7,6},{8,9},{9,8},{10,11... | collective-permute-start | bytes 1572872 | tf_op jit(solution)/shard_map/ppermute | solution.py:127
  414.7 35.7 %collective-permute-start.16 = (bf16[512,512]{1,0:T(8,128)(2,1)S(1)}, bf16[512,512]{1,0:T(8,128)(2,1)S(1)}, u32[]{:S(2)}, u32[]{:S(2)}) collective-permute-start(bf16[512,512]{1,0:T(8,128)(2,1)S(1)} %add_convert_fusion.4), channel_id=1, source_target_pairs={{0,4},{1,5},{2,6},{3,7},{4,0},{5,1},{6,2},{7,3},{8,12},{9,13},{10,... | collective-permute-start | bytes 1572872 | tf_op jit(solution)/shard_map/ppermute | solution.py:127
  418.1 21.9 %collective-permute-start.40 = (bf16[512,512]{1,0:T(8,128)(2,1)}, bf16[512,512]{1,0:T(8,128)(2,1)S(1)}, u32[]{:S(2)}, u32[]{:S(2)}) collective-permute-start(bf16[512,512]{1,0:T(8,128)(2,1)} %get-tuple-element.84), channel_id=1, source_target_pairs={{0,1},{1,0},{2,3},{3,2},{4,5},{5,4},{6,7},{7,6},{8,9},{9,8},{10,11... | collective-permute-start | bytes 1572872 | tf_op jit(solution)/shard_map/ppermute | solution.py:127
  418.8 27.3 %collective-permute-start.18 = (bf16[512,512]{1,0:T(8,128)(2,1)S(1)}, bf16[512,512]{1,0:T(8,128)(2,1)S(1)}, u32[]{:S(2)}, u32[]{:S(2)}) collective-permute-start(bf16[512,512]{1,0:T(8,128)(2,1)S(1)} %add_convert_fusion.3), channel_id=1, source_target_pairs={{0,2},{1,3},{2,0},{3,1},{4,6},{5,7},{6,4},{7,5},{8,10},{9,11},{10,... | collective-permute-start | bytes 1572872 | tf_op jit(solution)/shard_map/ppermute | solution.py:127
  428.7 17.2 %collective-permute-start.39 = (bf16[512,512]{1,0:T(8,128)(2,1)S(1)}, bf16[512,512]{1,0:T(8,128)(2,1)S(1)}, u32[]{:S(2)}, u32[]{:S(2)}) collective-permute-start(bf16[512,512]{1,0:T(8,128)(2,1)S(1)} %copy-done.29), channel_id=1, source_target_pairs={{0,1},{1,0},{2,3},{3,2},{4,5},{5,4},{6,7},{7,6},{8,9},{9,8},{10,11... | collective-permute-start | bytes 1572872 | tf_op jit(solution)/shard_map/ppermute | solution.py:127
  440.0 16.8 %collective-permute-start.38 = (bf16[512,512]{1,0:T(8,128)(2,1)}, bf16[512,512]{1,0:T(8,128)(2,1)}, u32[]{:S(2)}, u32[]{:S(2)}) collective-permute-start(bf16[512,512]{1,0:T(8,128)(2,1)} %get-tuple-element.80), channel_id=1, source_target_pairs={{0,1},{1,0},{2,3},{3,2},{4,5},{5,4},{6,7},{7,6},{8,9},{9,8},{10,11... | collective-permute-start | bytes 1572872 | tf_op jit(solution)/shard_map/ppermute | solution.py:127
  445.9 24.8 %collective-permute-start.42 = (bf16[512,512]{1,0:T(8,128)(2,1)S(1)}, bf16[512,512]{1,0:T(8,128)(2,1)}, u32[]{:S(2)}, u32[]{:S(2)}) collective-permute-start(bf16[512,512]{1,0:T(8,128)(2,1)S(1)} %add_convert_fusion.1), channel_id=1, source_target_pairs={{0,4},{1,5},{2,6},{3,7},{4,0},{5,1},{6,2},{7,3},{8,12},{9,13},{10,... | collective-permute-start | bytes 1572872 | tf_op jit(solution)/shard_map/ppermute | solution.py:127
  446.1 33.3 %collective-permute-start.43 = (bf16[512,512]{1,0:T(8,128)(2,1)S(1)}, bf16[512,512]{1,0:T(8,128)(2,1)}, u32[]{:S(2)}, u32[]{:S(2)}) collective-permute-start(bf16[512,512]{1,0:T(8,128)(2,1)S(1)} %add_convert_fusion.2), channel_id=1, source_target_pairs={{0,6},{1,7},{2,4},{3,5},{4,2},{5,3},{6,0},{7,1},{8,14},{9,15},{10,... | collective-permute-start | bytes 1572872 | tf_op jit(solution)/shard_map/ppermute | solution.py:127
  450.4 20.3 %collective-permute-start.44 = (bf16[512,512]{1,0:T(8,128)(2,1)S(1)}, bf16[512,512]{1,0:T(8,128)(2,1)}, u32[]{:S(2)}, u32[]{:S(2)}) collective-permute-start(bf16[512,512]{1,0:T(8,128)(2,1)S(1)} %add_convert_fusion), channel_id=1, source_target_pairs={{0,2},{1,3},{2,0},{3,1},{4,6},{5,7},{6,4},{7,5},{8,10},{9,11},{10,... | collective-permute-start | bytes 1572872 | tf_op jit(solution)/shard_map/ppermute | solution.py:127
  452.3 1.2 collective-permute-start.45
  453.5 2.8 collective-permute-start.46
  (33 other events, 838.6 us)

commit v2 on v1

--- a/solution.py
+++ b/solution.py
@@ -30,7 +30,7 @@
 
 def flash_kernel(use_ref, q_ref, *refs, blocks, bq, bk):
     k_refs, v_refs = refs[:blocks], refs[blocks : 2 * blocks]
-    o_ref, top_ref, m_s, l_s, acc_s = refs[2 * blocks :]
+    o_ref, top_ref, m_s, l_s, acc_s, k_s, v_s = refs[2 * blocks :]
     rows = q_ref.shape[0]
     turns = rows // bq
 
@@ -72,9 +72,17 @@
 
         @pl.when(use_ref[e] > 0)
         def _():
+            k_s[e - 1] = k_refs[e][...]
+            v_s[e - 1] = v_refs[e][...]
+
+    @pl.loop(1, blocks)
+    def _(e):
+        @pl.when(use_ref[e] > 0)
+        def _():
             for j in range(rows // bk):
+                at = pl.ds(j * bk, bk)
                 for i in range(turns):
-                    step(i, k_refs[e][pl.ds(j * bk, bk), :], v_refs[e][pl.ds(j * bk, bk), :], False)
+                    step(i, k_s[e - 1, at, :], v_s[e - 1, at, :], False)
 
     best = jnp.full((1, 128), NEG, jnp.float32)
     for i in range(turns):
@@ -91,7 +99,8 @@
     blocks = len(pairs)
     bq = min(BLOCK_Q, rows)
     bk = min(BLOCK_K, rows)
-    spec = pl.BlockSpec((rows, head), lambda h, f: (0, h + first))
+    spec = pl.BlockSpec((rows, head), lambda h, f: (0, h + f[blocks]))
+    use = jnp.concatenate([use, jnp.full((1,), first, jnp.int32)])
     made = pl.BlockSpec((rows, head), lambda h, f: (0, h))
     second = pl.BlockSpec((rows, head), lambda h, f: (0, h + heads))
     return pl.pallas_call(
@@ -105,6 +114,8 @@
                 pltpu.VMEM((rows, 128), jnp.float32),
                 pltpu.VMEM((rows, 128), jnp.float32),
                 pltpu.VMEM((rows, head), jnp.float32),
+                pltpu.VMEM((blocks - 1, rows, head), jnp.bfloat16),
+                pltpu.VMEM((blocks - 1, rows, head), jnp.bfloat16),
             ],
         ),
         out_shape=[

time: 491 us -> 483 us (0.984); the launches traced: 483 us -> 482 us
  no operation moved by 1% of the time
where the time goes in v2:
time: 483 us; the launch traced here: 482 us
  Pallas kernels  255 us (53%)
  waiting for transfers between devices  135 us (28%)
  starting transfers between devices  67.1 us (14%)
  other arithmetic  12.1 us (3%)
  local copies, waits for them, and re-layouts  11.8 us (2%)
    pallas_call x1, Pallas kernels, gather_first(): pl.pallas_call(functools.partial(gather_kernel, line=line), in_specs=[pl....  95.3 us
    pallas_call x3, Pallas kernels, project(): pl.pallas_call(functools.partial(project_kernel, plan=plan, parts=parts,...  72.5 us
    ppermute x32, waiting for transfers between devices, swapped(): return lax.ppermute(value, axis, [(i, i ^ bit) for i in range(size)])  63.1 us
    pallas_call x4, Pallas kernels, flash(): pl.pallas_call(functools.partial(flash_kernel, blocks=blocks, bq=bq, bk=b...  61 us
    ppermute x4, waiting for transfers between devices, earlier_blocks(): lax.ppermute(block, 'seq', [(i, i + across * d) for i in range(count - ac...  48.7 us
    ppermute x32, starting transfers between devices, swapped(): return lax.ppermute(value, axis, [(i, i ^ bit) for i in range(size)])  40 us
    pallas_call x2, Pallas kernels, combine(): pl.pallas_call(functools.partial(combine_kernel, groups=groups, blocks=le...  26.5 us
    ppermute x11, waiting for transfers between devices, moved(): return lax.ppermute(value, 'tensor', pairs)  22.8 us
  transfers between devices with their start and end apart: 47, of which 13 were waited for; matrix products, arithmetic and copies ran while one was open for 3% of the time, Pallas kernels for 27%

profile of v2, /device:TPU:11, one launch (start us, length us, event | category | flops | bytes accessed | tf_op | source)
XLA Modules:
  0.0 482.2 jit_solution(10069706124109788572)
XLA Ops:
  0.7 95.3 %shard_map.76 = (bf16[8,1024,512]{2,1,0:T(8,128)(2,1)}, bf16[1024,512]{1,0:T(8,128)(2,1)}, bf16[1024,512]{1,0:T(8,128)(2,1)}, bf16[1024,512]{1,0:T(8,128)(2,1)}) custom-call(bf16[2,1024,512]{2,1,0:T(8,128)(2,1)} %tok_ref.1), custom_call_target="tpu_custom_call" | custom-call | flops 89999998976 | bytes 8388608 | tf_op jit(solution)/shard_map/pallas_call | solution.py:286
  96.1 1.9 fusion
  98.6 1.4 pad_maximum_fusion.1
  100.0 28.6 %shard_map.77 = (bf16[1024,512]{1,0:T(8,128)(2,1)}, bf16[1024,512]{1,0:T(8,128)(2,1)}, bf16[1024,512]{1,0:T(8,128)(2,1)}, f32[2,8,1024]{2,1,0:T(8,128)}) custom-call(bf16[8,1024,512]{2,1,0:T(8,128)(2,1)} %get-tuple-element.50.refs_0_, bf16[3,4096,512]{2,1,0:T(8,128)(2,1)} %bitcast.12, f32[2,512]{1,0:T(2,128)} %pad_maximum_fusion.4.refs_2_, ...), custom_call_target="tpu_custom_call" | custom-call | flops 12884901888 | bytes 26214400 | tf_op jit(solution)/shard_map/pallas_call | solution.py:501
  129.9 2.2 collective-permute-start.3
  133.4 3.4 collective-permute-start.20
  136.8 16.6 %collective-permute-done.4.refs_2_.refs_6_ = bf16[1024,512]{1,0:T(8,128)(2,1)} collective-permute-done((bf16[1024,512]{1,0:T(8,128)(2,1)}, bf16[1024,512]{1,0:T(8,128)(2,1)}, u32[]{:S(2)}, u32[]{:S(2)}) %collective-permute-start.4) | collective-permute-done | bytes 1048608 | tf_op jit(solution)/shard_map/ppermute | solution.py:143
  153.4 1.9 collective-permute-start.21
  155.3 2.3 collective-permute-start.22
  157.6 18.2 %collective-permute-done.1.refs_2_.refs_6_ = bf16[1024,512]{1,0:T(8,128)(2,1)} collective-permute-done((bf16[1024,512]{1,0:T(8,128)(2,1)}, bf16[1024,512]{1,0:T(8,128)(2,1)}, u32[]{:S(2)}, u32[]{:S(2)}) %collective-permute-start.1) | collective-permute-done | bytes 1048608 | tf_op jit(solution)/shard_map/ppermute | solution.py:143
  175.9 1.9 collective-permute-start.23
  177.8 1.9 collective-permute-start.19
  179.7 3.4 collective-permute-start.5
  183.1 2.4 collective-permute-start.2
  186.2 13.4 %collective-permute-done.23.refs_7_ = bf16[1024,512]{1,0:T(8,128)(2,1)} collective-permute-done((bf16[1024,512]{1,0:T(8,128)(2,1)S(1)}, bf16[1024,512]{1,0:T(8,128)(2,1)}, u32[]{:S(2)}, u32[]{:S(2)}) %collective-permute-start.23) | collective-permute-done | bytes 1048608 | tf_op jit(solution)/shard_map/ppermute | solution.py:307
  199.6 2.2 collective-permute-start.27
  203.2 2.3 constant_dynamic-slice_fusion.2
  206.2 3.7 collective-permute-start.25
  209.9 1.6 collective-permute-start.28
  211.6 9.4 %collective-permute-done.27.refs_11_ = bf16[1024,512]{1,0:T(8,128)(2,1)S(1)} collective-permute-done((bf16[1024,512]{1,0:T(8,128)(2,1)}, bf16[1024,512]{1,0:T(8,128)(2,1)S(1)}, u32[]{:S(2)}, u32[]{:S(2)}) %collective-permute-start.27) | collective-permute-done | bytes 1048608 | tf_op jit(solution)/shard_map/ppermute | solution.py:307
  221.0 1.6 collective-permute-start.29
  222.6 15.2 %shard_map.79 = (bf16[1024,256]{1,0:T(8,128)(2,1)}, f32[2,8,128]{2,1,0:T(8,128)}) custom-call(s32[5]{0:T(128)} %concatenate.51.use_ref, bf16[1024,512]{1,0:T(8,128)(2,1)} %get-tuple-element.51.q_ref, bf16[1024,512]{1,0:T(8,128)(2,1)} %get-tuple-element.54.refs_0_.refs_4_, bf16[1024,512]{1,0:T(8,128)(2,1)} %copy-done.27, ...), custom_call_target="tpu_custom_call" | custom-call | flops 8589934592 | bytes 4194304 | tf_op jit(solution)/shard_map/pallas_call | solution.py:106
  237.8 15.3 %shard_map.78 = (bf16[1024,256]{1,0:T(8,128)(2,1)}, f32[2,8,128]{2,1,0:T(8,128)}) custom-call(s32[5]{0:T(128)} %concatenate.47.use_ref, bf16[1024,512]{1,0:T(8,128)(2,1)} %get-tuple-element.51.q_ref, bf16[1024,512]{1,0:T(8,128)(2,1)} %get-tuple-element.52.refs_0_.refs_4_, bf16[1024,512]{1,0:T(8,128)(2,1)} %copy-done.28, ...), custom_call_target="tpu_custom_call" | custom-call | flops 8589934592 | bytes 4194304 | tf_op jit(solution)/shard_map/pallas_call | solution.py:106
  253.2 2.4 collective-permute-start.9
  255.7 20.7 %shard_map.82 = (bf16[1024,512]{1,0:T(8,128)(2,1)}, bf16[1024,512]{1,0:T(8,128)(2,1)}, f32[1,8,1024]{2,1,0:T(8,128)}) custom-call(bf16[1024,512]{1,0:T(8,128)(2,1)} %get-tuple-element.67.refs_0_, bf16[1024,512]{1,0:T(8,128)(2,1)} %collective-permute-done.19.refs_1_, bf16[1024,512]{1,0:T(8,128)(2,1)} %get-tuple-element.71.refs_2_, ...), custom_call_target="tpu_custom_call" | custom-call | flops 8589934592 | bytes 26214400 | tf_op jit(solution)/shard_map/pallas_call | solution.py:501
  277.7 1.8 collective-permute-start.11
  281.2 4.1 collective-permute-start.7
  287.6 13.9 %collective-permute-done.34.refs_2_.refs_6_ = bf16[1024,512]{1,0:T(8,128)(2,1)S(1)} collective-permute-done((bf16[1024,512]{1,0:T(8,128)(2,1)}, bf16[1024,512]{1,0:T(8,128)(2,1)S(1)}, u32[]{:S(2)}, u32[]{:S(2)}) %collective-permute-start.34) | collective-permute-done | bytes 1048608 | tf_op jit(solution)/shard_map/ppermute | solution.py:143
  301.4 4.7 collective-permute-start.35
  308.1 2.4 collective-permute-start.6
  310.5 23.3 %shard_map.81 = (bf16[1024,512]{1,0:T(8,128)(2,1)}, f32[1,8,1024]{2,1,0:T(8,128)}) custom-call(bf16[1024,512]{1,0:T(8,128)(2,1)} %get-tuple-element.67.refs_0_, bf16[1024,512]{1,0:T(8,128)(2,1)} %collective-permute-done.19.refs_1_, bf16[1024,512]{1,0:T(8,128)(2,1)} %get-tuple-element.71.refs_2_, bf16[1024,512]{1,0:T(8,128)(2,1)} %get-tuple-element.72.refs_3_, ...), custom_call_target="tpu_custom_call" | custom-call | flops 4294967296 | bytes 26214400 | tf_op jit(solution)/shard_map/pallas_call | solution.py:501
  336.3 13.3 %shard_map.80 = (bf16[512,512]{1,0:T(8,128)(2,1)}, bf16[512,512]{1,0:T(8,128)(2,1)}, bf16[512,512]{1,0:T(8,128)(2,1)}, bf16[512,512]{1,0:T(8,128)(2,1)}, bf16[51...) custom-call(s32[3]{0:T(128)} %pad_add_fusion.where_ref, ...), custom_call_target="tpu_custom_call" | custom-call | flops 4294967296 | bytes 16777216 | tf_op jit(solution)/shard_map/pallas_call | solution.py:578
  353.4 15.3 %shard_map.84 = (bf16[1024,256]{1,0:T(8,128)(2,1)}, f32[2,8,128]{2,1,0:T(8,128)}) custom-call(s32[5]{0:T(128)} %concatenate.51.use_ref, bf16[1024,512]{1,0:T(8,128)(2,1)} %get-tuple-element.74.q_ref, bf16[1024,512]{1,0:T(8,128)(2,1)} %get-tuple-element.77.refs_0_.refs_4_, bf16[1024,512]{1,0:T(8,128)(2,1)} %collective-permute-done.33.refs_1_.refs_5_, ...), custom_call_target="tpu_custom_call" | custom-call | flops 8589934592 | bytes 4194304 | tf_op jit(solution)/shard_map/pallas_call | solution.py:106
  370.3 15.2 %shard_map.83 = (bf16[1024,256]{1,0:T(8,128)(2,1)}, f32[2,8,128]{2,1,0:T(8,128)}) custom-call(s32[5]{0:T(128)} %concatenate.47.use_ref, bf16[1024,512]{1,0:T(8,128)(2,1)} %get-tuple-element.74.q_ref, bf16[1024,512]{1,0:T(8,128)(2,1)} %get-tuple-element.75.refs_0_.refs_4_, bf16[1024,512]{1,0:T(8,128)(2,1)} %collective-permute-done.30.refs_1_.refs_5_, ...), custom_call_target="tpu_custom_call" | custom-call | flops 8589934592 | bytes 4194304 | tf_op jit(solution)/shard_map/pallas_call | solution.py:106
  386.5 1.5 collective-permute-start.36
  388.3 12.5 %collective-permute-done.36.refs_2_ = bf16[512,256]{1,0:T(8,128)(2,1)S(1)} collective-permute-done((bf16[512,256]{1,0:T(8,128)(2,1)S(1)}, bf16[512,256]{1,0:T(8,128)(2,1)S(1)}, u32[]{:S(2)}, u32[]{:S(2)}) %collective-permute-start.36) | collective-permute-done | bytes 262176 | tf_op jit(solution)/shard_map/ppermute | solution.py:138
  401.5 13.2 %shard_map.85 = (bf16[512,512]{1,0:T(8,128)(2,1)}, bf16[512,512]{1,0:T(8,128)(2,1)}, bf16[512,512]{1,0:T(8,128)(2,1)}, bf16[512,512]{1,0:T(8,128)(2,1)}, bf16[51...) custom-call(s32[3]{0:T(128)} %pad_add_fusion.where_ref, ...), custom_call_target="tpu_custom_call" | custom-call | flops 4294967296 | bytes 16777216 | tf_op jit(solution)/shard_map/pallas_call | solution.py:578
  415.8 2.6 collective-permute-start.16
  419.1 9.8 %collective-permute-done.41 = bf16[512,512]{1,0:T(8,128)(2,1)S(1)} collective-permute-done((bf16[512,512]{1,0:T(8,128)(2,1)}, bf16[512,512]{1,0:T(8,128)(2,1)S(1)}, u32[]{:S(2)}, u32[]{:S(2)}) %collective-permute-start.41) | collective-permute-done | bytes 524320 | tf_op jit(solution)/shard_map/ppermute | solution.py:138
  430.0 10.2 %collective-permute-done.40 = bf16[512,512]{1,0:T(8,128)(2,1)S(1)} collective-permute-done((bf16[512,512]{1,0:T(8,128)(2,1)}, bf16[512,512]{1,0:T(8,128)(2,1)S(1)}, u32[]{:S(2)}, u32[]{:S(2)}) %collective-permute-start.40) | collective-permute-done | bytes 524320 | tf_op jit(solution)/shard_map/ppermute | solution.py:138
  441.2 4.5 collective-permute-done.39
  445.9 4.3 collective-permute-start.43
  450.3 1.5 select_convert_fusion.3
  453.3 2.8 collective-permute-done.46
  456.7 14.8 %collective-permute-done.44 = bf16[512,512]{1,0:T(8,128)(2,1)} collective-permute-done((bf16[512,512]{1,0:T(8,128)(2,1)S(1)}, bf16[512,512]{1,0:T(8,128)(2,1)}, u32[]{:S(2)}, u32[]{:S(2)}) %collective-permute-start.44) | collective-permute-done | bytes 524320 | tf_op jit(solution)/shard_map/ppermute | solution.py:138
  471.4 7.3 %collective-permute-done.43 = bf16[512,512]{1,0:T(8,128)(2,1)} collective-permute-done((bf16[512,512]{1,0:T(8,128)(2,1)S(1)}, bf16[512,512]{1,0:T(8,128)(2,1)}, u32[]{:S(2)}, u32[]{:S(2)}) %collective-permute-start.43) | collective-permute-done | bytes 524320 | tf_op jit(solution)/shard_map/ppermute | solution.py:138
  478.7 1.9 select_convert_fusion.1
  480.7 1.5 pad_maximum_fusion
  (162 shorter events, 29.4 us)
Async XLA Ops:
  0.7 97.3 %copy-start.24 = (f32[512]{0:T(512)S(1)}, f32[512]{0:T(512)}, u32[]{:S(2)}) copy-start(f32[512]{0:T(512)} %param.8) | copy-start | bytes 6148
  128.6 24.8 %collective-permute-start.4 = (bf16[1024,512]{1,0:T(8,128)(2,1)}, bf16[1024,512]{1,0:T(8,128)(2,1)}, u32[]{:S(2)}, u32[]{:S(2)}) collective-permute-start(bf16[1024,512]{1,0:T(8,128)(2,1)} %get-tuple-element.54.refs_0_.refs_4_), channel_id=1, source_target_pairs={{0,16},{8,24},{1,17},{9,25},{2,18},{10,26},{3,19},{11,27},{4,20},{... | collective-permute-start | bytes 3145736 | tf_op jit(solution)/shard_map/ppermute | solution.py:143
  129.9 25.4 %collective-permute-start.3 = (bf16[1024,512]{1,0:T(8,128)(2,1)}, bf16[1024,512]{1,0:T(8,128)(2,1)S(1)}, u32[]{:S(2)}, u32[]{:S(2)}) collective-permute-start(bf16[1024,512]{1,0:T(8,128)(2,1)} %get-tuple-element.54.refs_0_.refs_4_), channel_id=1, source_target_pairs={{0,8},{8,0},{16,24},{24,16},{1,9},{9,1},{17,25},{25,17},{2,10},{10... | collective-permute-start | bytes 3145736 | tf_op jit(solution)/shard_map/ppermute | solution.py:138
  132.0 43.8 %collective-permute-start.1 = (bf16[1024,512]{1,0:T(8,128)(2,1)}, bf16[1024,512]{1,0:T(8,128)(2,1)}, u32[]{:S(2)}, u32[]{:S(2)}) collective-permute-start(bf16[1024,512]{1,0:T(8,128)(2,1)} %get-tuple-element.52.refs_0_.refs_4_), channel_id=1, source_target_pairs={{0,16},{8,24},{1,17},{9,25},{2,18},{10,26},{3,19},{11,27},{4,20},{... | collective-permute-start | bytes 3145736 | tf_op jit(solution)/shard_map/ppermute | solution.py:143
  133.3 44.5 %collective-permute-start = (bf16[1024,512]{1,0:T(8,128)(2,1)}, bf16[1024,512]{1,0:T(8,128)(2,1)S(1)}, u32[]{:S(2)}, u32[]{:S(2)}) collective-permute-start(bf16[1024,512]{1,0:T(8,128)(2,1)} %get-tuple-element.52.refs_0_.refs_4_), channel_id=1, source_target_pairs={{0,8},{8,0},{16,24},{24,16},{1,9},{9,1},{17,25},{25,17},{2,10},{10... | collective-permute-start | bytes 3145736 | tf_op jit(solution)/shard_map/ppermute | solution.py:138
  133.4 46.3 %collective-permute-start.20 = (bf16[1024,512]{1,0:T(8,128)(2,1)S(1)}, bf16[1024,512]{1,0:T(8,128)(2,1)S(1)}, u32[]{:S(2)}, u32[]{:S(2)}) collective-permute-start(bf16[1024,512]{1,0:T(8,128)(2,1)S(1)} %copy-done.1), channel_id=1, source_target_pairs={{2,3},{3,2},{4,5},{5,4},{6,7},{7,6},{10,11},{11,10},{12,13},{13,12... | collective-permute-start | bytes 3145736 | tf_op jit(solution)/shard_map/ppermute | solution.py:307
  153.4 29.7 %collective-permute-start.21 = (bf16[1024,512]{1,0:T(8,128)(2,1)S(1)}, bf16[1024,512]{1,0:T(8,128)(2,1)S(1)}, u32[]{:S(2)}, u32[]{:S(2)}) collective-permute-start(bf16[1024,512]{1,0:T(8,128)(2,1)S(1)} %copy-done.2), channel_id=1, source_target_pairs={{0,1},{1,0},{2,3},{3,2},{4,5},{5,4},{8,9},{9,8},{10,11},{11,10},{1... | collective-permute-start | bytes 3145736 | tf_op jit(solution)/shard_map/ppermute | solution.py:307
  155.3 30.2 %collective-permute-start.22 = (bf16[1024,512]{1,0:T(8,128)(2,1)S(1)}, bf16[1024,512]{1,0:T(8,128)(2,1)}, u32[]{:S(2)}, u32[]{:S(2)}) collective-permute-start(bf16[1024,512]{1,0:T(8,128)(2,1)S(1)} %copy-done.1), channel_id=1, source_target_pairs={{2,4},{3,5},{4,6},{5,7},{10,12},{11,13},{12,14},{13,15},{18,20},{1... | collective-permute-start | bytes 3145736 | tf_op jit(solution)/shard_map/ppermute | solution.py:307
  175.9 23.7 %collective-permute-start.23 = (bf16[1024,512]{1,0:T(8,128)(2,1)S(1)}, bf16[1024,512]{1,0:T(8,128)(2,1)}, u32[]{:S(2)}, u32[]{:S(2)}) collective-permute-start(bf16[1024,512]{1,0:T(8,128)(2,1)S(1)} %copy-done.2), channel_id=1, source_target_pairs={{2,0},{3,1},{4,2},{5,3},{10,8},{11,9},{12,10},{13,11},{18,16},{19,... | collective-permute-start | bytes 3145736 | tf_op jit(solution)/shard_map/ppermute | solution.py:307
  177.8 27.6 %collective-permute-start.19 = (bf16[1024,512]{1,0:T(8,128)(2,1)S(1)}, bf16[1024,512]{1,0:T(8,128)(2,1)}, u32[]{:S(2)}, u32[]{:S(2)}) collective-permute-start(bf16[1024,512]{1,0:T(8,128)(2,1)S(1)} %copy-done), channel_id=1, source_target_pairs={{0,1},{1,0},{2,3},{3,2},{4,5},{5,4},{6,7},{7,6},{8,9},{9,8},{10,11... | collective-permute-start | bytes 3145736 | tf_op jit(solution)/shard_map/ppermute | solution.py:307
  179.7 25.8 %collective-permute-start.5 = (bf16[1024,512]{1,0:T(8,128)(2,1)}, bf16[1024,512]{1,0:T(8,128)(2,1)}, u32[]{:S(2)}, u32[]{:S(2)}) collective-permute-start(bf16[1024,512]{1,0:T(8,128)(2,1)} %collective-permute-done.4.refs_2_.refs_6_), channel_id=1, source_target_pairs={{0,8},{8,0},{16,24},{24,16},{1,9},{9,1},{17,25},{25,17},{2,10},{10... | collective-permute-start | bytes 3145736 | tf_op jit(solution)/shard_map/ppermute | solution.py:138
  183.1 23.2 %collective-permute-start.2 = (bf16[1024,512]{1,0:T(8,128)(2,1)}, bf16[1024,512]{1,0:T(8,128)(2,1)}, u32[]{:S(2)}, u32[]{:S(2)}) collective-permute-start(bf16[1024,512]{1,0:T(8,128)(2,1)} %collective-permute-done.1.refs_2_.refs_6_), channel_id=1, source_target_pairs={{0,8},{8,0},{16,24},{24,16},{1,9},{9,1},{17,25},{25,17},{2,10},{10... | collective-permute-start | bytes 3145736 | tf_op jit(solution)/shard_map/ppermute | solution.py:138
  185.5 24.4 %collective-permute-start.26 = (bf16[1024,512]{1,0:T(8,128)(2,1)}, bf16[1024,512]{1,0:T(8,128)(2,1)S(1)}, u32[]{:S(2)}, u32[]{:S(2)}) collective-permute-start(bf16[1024,512]{1,0:T(8,128)(2,1)} %collective-permute-done.22.refs_6_), channel_id=1, source_target_pairs={{4,6},{5,7},{12,14},{13,15},{20,22},{21,23},{28,30},{29,31}} | collective-permute-start | bytes 3145736 | tf_op jit(solution)/shard_map/ppermute | solution.py:307
  199.6 21.3 %collective-permute-start.27 = (bf16[1024,512]{1,0:T(8,128)(2,1)}, bf16[1024,512]{1,0:T(8,128)(2,1)S(1)}, u32[]{:S(2)}, u32[]{:S(2)}) collective-permute-start(bf16[1024,512]{1,0:T(8,128)(2,1)} %collective-permute-done.23.refs_7_), channel_id=1, source_target_pairs={{2,0},{3,1},{10,8},{11,9},{18,16},{19,17},{26,24},{27,25}} | collective-permute-start | bytes 3145736 | tf_op jit(solution)/shard_map/ppermute | solution.py:307
  205.5 47.7 %collective-permute-start.8 = (bf16[128,4096]{1,0:T(8,128)(2,1)}, bf16[128,4096]{1,0:T(8,128)(2,1)}, u32[]{:S(2)}, u32[]{:S(2)}) collective-permute-start(bf16[128,4096]{1,0:T(8,128)(2,1)} %constant_dynamic-slice_fusion.2), channel_id=1, source_target_pairs={{0,2},{1,3},{2,0},{3,1},{4,6},{5,7},{6,4},{7,5},{8,10},{9,11},{10,... | collective-permute-start | bytes 3145736 | tf_op jit(solution)/shard_map/ppermute | solution.py:138
  205.5 47.7 %collective-permute-start.24 = (bf16[1024,512]{1,0:T(8,128)(2,1)}, bf16[1024,512]{1,0:T(8,128)(2,1)S(1)}, u32[]{:S(2)}, u32[]{:S(2)}) collective-permute-start(bf16[1024,512]{1,0:T(8,128)(2,1)} %collective-permute-done.22.refs_6_), channel_id=1, source_target_pairs={{4,5},{5,4},{6,7},{7,6},{12,13},{13,12},{14,15},{15,14},{20,21},{2... | collective-permute-start | bytes 3145736 | tf_op jit(solution)/shard_map/ppermute | solution.py:307
  206.2 49.4 %collective-permute-start.25 = (bf16[1024,512]{1,0:T(8,128)(2,1)}, bf16[1024,512]{1,0:T(8,128)(2,1)}, u32[]{:S(2)}, u32[]{:S(2)}) collective-permute-start(bf16[1024,512]{1,0:T(8,128)(2,1)} %collective-permute-done.23.refs_7_), channel_id=1, source_target_pairs={{0,1},{1,0},{2,3},{3,2},{8,9},{9,8},{10,11},{11,10},{16,17},{17,16... | collective-permute-start | bytes 3145736 | tf_op jit(solution)/shard_map/ppermute | solution.py:307
  209.9 45.7 %collective-permute-start.28 = (bf16[1024,512]{1,0:T(8,128)(2,1)S(1)}, bf16[1024,512]{1,0:T(8,128)(2,1)}, u32[]{:S(2)}, u32[]{:S(2)}) collective-permute-start(bf16[1024,512]{1,0:T(8,128)(2,1)S(1)} %collective-permute-done.26.refs_10_), channel_id=1, source_target_pairs={{6,7},{7,6},{14,15},{15,14},{22,23},{23,22},{30,31},{31,30}} | collective-permute-start | bytes 3145736 | tf_op jit(solution)/shard_map/ppermute | solution.py:307
  221.0 34.7 %collective-permute-start.29 = (bf16[1024,512]{1,0:T(8,128)(2,1)S(1)}, bf16[1024,512]{1,0:T(8,128)(2,1)}, u32[]{:S(2)}, u32[]{:S(2)}) collective-permute-start(bf16[1024,512]{1,0:T(8,128)(2,1)S(1)} %collective-permute-done.27.refs_11_), channel_id=1, source_target_pairs={{0,1},{1,0},{8,9},{9,8},{16,17},{17,16},{24,25},{25,24}} | collective-permute-start | bytes 3145736 | tf_op jit(solution)/shard_map/ppermute | solution.py:307
  253.1 24.5 %collective-permute-start.10 = (bf16[128,4096]{1,0:T(8,128)(2,1)}, bf16[128,4096]{1,0:T(8,128)(2,1)}, u32[]{:S(2)}, u32[]{:S(2)}) collective-permute-start(bf16[128,4096]{1,0:T(8,128)(2,1)} %collective-permute-done.8.refs_5_), channel_id=1, source_target_pairs={{0,16},{8,24},{16,0},{24,8},{1,17},{9,25},{17,1},{25,9},{2,18},{10... | collective-permute-start | bytes 3145736 | tf_op jit(solution)/shard_map/ppermute | solution.py:138
  253.2 34.0 %collective-permute-start.9 = (bf16[128,4096]{1,0:T(8,128)(2,1)}, bf16[128,4096]{1,0:T(8,128)(2,1)}, u32[]{:S(2)}, u32[]{:S(2)}) collective-permute-start(bf16[128,4096]{1,0:T(8,128)(2,1)} %collective-permute-done.8.refs_5_), channel_id=1, source_target_pairs={{0,8},{8,0},{16,24},{24,16},{1,9},{9,1},{17,25},{25,17},{2,10},{10... | collective-permute-start | bytes 3145736 | tf_op jit(solution)/shard_map/ppermute | solution.py:138
  276.3 25.1 %collective-permute-start.34 = (bf16[1024,512]{1,0:T(8,128)(2,1)}, bf16[1024,512]{1,0:T(8,128)(2,1)S(1)}, u32[]{:S(2)}, u32[]{:S(2)}) collective-permute-start(bf16[1024,512]{1,0:T(8,128)(2,1)} %get-tuple-element.77.refs_0_.refs_4_), channel_id=1, source_target_pairs={{0,16},{8,24},{1,17},{9,25},{2,18},{10,26},{3,19},{11,27},{4,20},{... | collective-permute-start | bytes 3145736 | tf_op jit(solution)/shard_map/ppermute | solution.py:143
  277.7 57.4 %collective-permute-start.11 = (bf16[128,4096]{1,0:T(8,128)(2,1)}, bf16[128,4096]{1,0:T(8,128)(2,1)S(1)}, u32[]{:S(2)}, u32[]{:S(2)}) collective-permute-start(bf16[128,4096]{1,0:T(8,128)(2,1)} %collective-permute-done.10.refs_7_), channel_id=1, source_target_pairs={{0,8},{8,0},{16,24},{24,16},{1,9},{9,1},{17,25},{25,17},{2,10},{10... | collective-permute-start | bytes 3145736 | tf_op jit(solution)/shard_map/ppermute | solution.py:138
  281.2 26.9 %collective-permute-start.7 = (bf16[512,256]{1,0:T(8,128)(2,1)S(1)}, bf16[512,256]{1,0:T(8,128)(2,1)S(1)}, u32[]{:S(2)}, u32[]{:S(2)}) collective-permute-start(bf16[512,256]{1,0:T(8,128)(2,1)S(1)} %constant_dynamic-slice_fusion.3), channel_id=1, source_target_pairs={{0,2},{1,3},{2,0},{3,1},{4,6},{5,7},{6,4},{7,5},{8,10},{9,11},{10,... | collective-permute-start | bytes 786440 | tf_op jit(solution)/shard_map/ppermute | solution.py:138
  285.3 65.3 %collective-permute-start.31 = (bf16[1024,512]{1,0:T(8,128)(2,1)}, bf16[1024,512]{1,0:T(8,128)(2,1)}, u32[]{:S(2)}, u32[]{:S(2)}) collective-permute-start(bf16[1024,512]{1,0:T(8,128)(2,1)} %get-tuple-element.75.refs_0_.refs_4_), channel_id=1, source_target_pairs={{0,16},{8,24},{1,17},{9,25},{2,18},{10,26},{3,19},{11,27},{4,20},{... | collective-permute-start | bytes 3145736 | tf_op jit(solution)/shard_map/ppermute | solution.py:143
  287.2 64.7 %collective-permute-start.33 = (bf16[1024,512]{1,0:T(8,128)(2,1)}, bf16[1024,512]{1,0:T(8,128)(2,1)}, u32[]{:S(2)}, u32[]{:S(2)}) collective-permute-start(bf16[1024,512]{1,0:T(8,128)(2,1)} %get-tuple-element.77.refs_0_.refs_4_), channel_id=1, source_target_pairs={{0,8},{8,0},{16,24},{24,16},{1,9},{9,1},{17,25},{25,17},{2,10},{10... | collective-permute-start | bytes 3145736 | tf_op jit(solution)/shard_map/ppermute | solution.py:138
  301.4 51.0 %collective-permute-start.35 = (bf16[1024,512]{1,0:T(8,128)(2,1)S(1)}, bf16[1024,512]{1,0:T(8,128)(2,1)}, u32[]{:S(2)}, u32[]{:S(2)}) collective-permute-start(bf16[1024,512]{1,0:T(8,128)(2,1)S(1)} %collective-permute-done.34.refs_2_.refs_6_), channel_id=1, source_target_pairs={{0,8},{8,0},{16,24},{24,16},{1,9},{9,1},{17,25},{25,17},{2,10},{10... | collective-permute-start | bytes 3145736 | tf_op jit(solution)/shard_map/ppermute | solution.py:138
  308.1 26.5 %collective-permute-start.6 = (bf16[512,256]{1,0:T(8,128)(2,1)S(1)}, bf16[512,256]{1,0:T(8,128)(2,1)S(1)}, u32[]{:S(2)}, u32[]{:S(2)}) collective-permute-start(bf16[512,256]{1,0:T(8,128)(2,1)S(1)} %constant_dynamic-slice_fusion.4), channel_id=1, source_target_pairs={{0,2},{1,3},{2,0},{3,1},{4,6},{5,7},{6,4},{7,5},{8,10},{9,11},{10,... | collective-permute-start | bytes 786440 | tf_op jit(solution)/shard_map/ppermute | solution.py:138
  334.6 35.0 %collective-permute-start.30 = (bf16[1024,512]{1,0:T(8,128)(2,1)}, bf16[1024,512]{1,0:T(8,128)(2,1)}, u32[]{:S(2)}, u32[]{:S(2)}) collective-permute-start(bf16[1024,512]{1,0:T(8,128)(2,1)} %get-tuple-element.75.refs_0_.refs_4_), channel_id=1, source_target_pairs={{0,8},{8,0},{16,24},{24,16},{1,9},{9,1},{17,25},{25,17},{2,10},{10... | collective-permute-start | bytes 3145736 | tf_op jit(solution)/shard_map/ppermute | solution.py:138
  349.6 36.9 %collective-permute-start.15 = (bf16[512,512]{1,0:T(8,128)(2,1)}, bf16[512,512]{1,0:T(8,128)(2,1)S(1)}, u32[]{:S(2)}, u32[]{:S(2)}) collective-permute-start(bf16[512,512]{1,0:T(8,128)(2,1)} %get-tuple-element.63), channel_id=1, source_target_pairs={{0,1},{1,0},{2,3},{3,2},{4,5},{5,4},{6,7},{7,6},{8,9},{9,8},{10,11... | collective-permute-start | bytes 1572872 | tf_op jit(solution)/shard_map/ppermute | solution.py:138
  350.5 19.7 %collective-permute-start.32 = (bf16[1024,512]{1,0:T(8,128)(2,1)}, bf16[1024,512]{1,0:T(8,128)(2,1)}, u32[]{:S(2)}, u32[]{:S(2)}) collective-permute-start(bf16[1024,512]{1,0:T(8,128)(2,1)} %collective-permute-done.31.refs_2_.refs_6_), channel_id=1, source_target_pairs={{0,8},{8,0},{16,24},{24,16},{1,9},{9,1},{17,25},{25,17},{2,10},{10... | collective-permute-start | bytes 3145736 | tf_op jit(solution)/shard_map/ppermute | solution.py:138
  351.9 36.3 %collective-permute-start.14 = (bf16[512,512]{1,0:T(8,128)(2,1)}, bf16[512,512]{1,0:T(8,128)(2,1)S(1)}, u32[]{:S(2)}, u32[]{:S(2)}) collective-permute-start(bf16[512,512]{1,0:T(8,128)(2,1)} %get-tuple-element.61), channel_id=1, source_target_pairs={{0,1},{1,0},{2,3},{3,2},{4,5},{5,4},{6,7},{7,6},{8,9},{9,8},{10,11... | collective-permute-start | bytes 1572872 | tf_op jit(solution)/shard_map/ppermute | solution.py:138
  352.5 65.9 %collective-permute-start.13 = (bf16[512,512]{1,0:T(8,128)(2,1)}, bf16[512,512]{1,0:T(8,128)(2,1)S(1)}, u32[]{:S(2)}, u32[]{:S(2)}) collective-permute-start(bf16[512,512]{1,0:T(8,128)(2,1)} %get-tuple-element.59), channel_id=1, source_target_pairs={{0,1},{1,0},{2,3},{3,2},{4,5},{5,4},{6,7},{7,6},{8,9},{9,8},{10,11... | collective-permute-start | bytes 1572872 | tf_op jit(solution)/shard_map/ppermute | solution.py:138
  369.6 49.3 %collective-permute-start.12 = (bf16[512,512]{1,0:T(8,128)(2,1)}, bf16[512,512]{1,0:T(8,128)(2,1)S(1)}, u32[]{:S(2)}, u32[]{:S(2)}) collective-permute-start(bf16[512,512]{1,0:T(8,128)(2,1)} %get-tuple-element.57), channel_id=1, source_target_pairs={{0,1},{1,0},{2,3},{3,2},{4,5},{5,4},{6,7},{7,6},{8,9},{9,8},{10,11... | collective-permute-start | bytes 1572872 | tf_op jit(solution)/shard_map/ppermute | solution.py:138
  370.3 18.0 %collective-permute-start.37 = (bf16[512,256]{1,0:T(8,128)(2,1)S(1)}, bf16[512,256]{1,0:T(8,128)(2,1)S(1)}, u32[]{:S(2)}, u32[]{:S(2)}) collective-permute-start(bf16[512,256]{1,0:T(8,128)(2,1)S(1)} %constant_dynamic-slice_fusion), channel_id=1, source_target_pairs={{0,2},{1,3},{2,0},{3,1},{4,6},{5,7},{6,4},{7,5},{8,10},{9,11},{10,... | collective-permute-start | bytes 786440 | tf_op jit(solution)/shard_map/ppermute | solution.py:138
  386.5 14.3 %collective-permute-start.36 = (bf16[512,256]{1,0:T(8,128)(2,1)S(1)}, bf16[512,256]{1,0:T(8,128)(2,1)S(1)}, u32[]{:S(2)}, u32[]{:S(2)}) collective-permute-start(bf16[512,256]{1,0:T(8,128)(2,1)S(1)} %constant_dynamic-slice_fusion.1), channel_id=1, source_target_pairs={{0,2},{1,3},{2,0},{3,1},{4,6},{5,7},{6,4},{7,5},{8,10},{9,11},{10,... | collective-permute-start | bytes 786440 | tf_op jit(solution)/shard_map/ppermute | solution.py:138
  388.2 62.0 %collective-permute-start.17 = (bf16[512,512]{1,0:T(8,128)(2,1)S(1)}, bf16[512,512]{1,0:T(8,128)(2,1)}, u32[]{:S(2)}, u32[]{:S(2)}) collective-permute-start(bf16[512,512]{1,0:T(8,128)(2,1)S(1)} %add_convert_fusion.5), channel_id=1, source_target_pairs={{0,6},{1,7},{2,4},{3,5},{4,2},{5,3},{6,0},{7,1},{8,14},{9,15},{10,... | collective-permute-start | bytes 1572872 | tf_op jit(solution)/shard_map/ppermute | solution.py:138
  414.7 14.2 %collective-permute-start.41 = (bf16[512,512]{1,0:T(8,128)(2,1)}, bf16[512,512]{1,0:T(8,128)(2,1)S(1)}, u32[]{:S(2)}, u32[]{:S(2)}) collective-permute-start(bf16[512,512]{1,0:T(8,128)(2,1)} %get-tuple-element.86), channel_id=1, source_target_pairs={{0,1},{1,0},{2,3},{3,2},{4,5},{5,4},{6,7},{7,6},{8,9},{9,8},{10,11... | collective-permute-start | bytes 1572872 | tf_op jit(solution)/shard_map/ppermute | solution.py:138
  415.8 34.4 %collective-permute-start.16 = (bf16[512,512]{1,0:T(8,128)(2,1)S(1)}, bf16[512,512]{1,0:T(8,128)(2,1)S(1)}, u32[]{:S(2)}, u32[]{:S(2)}) collective-permute-start(bf16[512,512]{1,0:T(8,128)(2,1)S(1)} %add_convert_fusion.4), channel_id=1, source_target_pairs={{0,4},{1,5},{2,6},{3,7},{4,0},{5,1},{6,2},{7,3},{8,12},{9,13},{10,... | collective-permute-start | bytes 1572872 | tf_op jit(solution)/shard_map/ppermute | solution.py:138
  418.3 21.9 %collective-permute-start.40 = (bf16[512,512]{1,0:T(8,128)(2,1)}, bf16[512,512]{1,0:T(8,128)(2,1)S(1)}, u32[]{:S(2)}, u32[]{:S(2)}) collective-permute-start(bf16[512,512]{1,0:T(8,128)(2,1)} %get-tuple-element.84), channel_id=1, source_target_pairs={{0,1},{1,0},{2,3},{3,2},{4,5},{5,4},{6,7},{7,6},{8,9},{9,8},{10,11... | collective-permute-start | bytes 1572872 | tf_op jit(solution)/shard_map/ppermute | solution.py:138
  419.0 26.8 %collective-permute-start.18 = (bf16[512,512]{1,0:T(8,128)(2,1)S(1)}, bf16[512,512]{1,0:T(8,128)(2,1)S(1)}, u32[]{:S(2)}, u32[]{:S(2)}) collective-permute-start(bf16[512,512]{1,0:T(8,128)(2,1)S(1)} %add_convert_fusion.3), channel_id=1, source_target_pairs={{0,2},{1,3},{2,0},{3,1},{4,6},{5,7},{6,4},{7,5},{8,10},{9,11},{10,... | collective-permute-start | bytes 1572872 | tf_op jit(solution)/shard_map/ppermute | solution.py:138
  428.9 16.8 %collective-permute-start.39 = (bf16[512,512]{1,0:T(8,128)(2,1)S(1)}, bf16[512,512]{1,0:T(8,128)(2,1)S(1)}, u32[]{:S(2)}, u32[]{:S(2)}) collective-permute-start(bf16[512,512]{1,0:T(8,128)(2,1)S(1)} %copy-done.29), channel_id=1, source_target_pairs={{0,1},{1,0},{2,3},{3,2},{4,5},{5,4},{6,7},{7,6},{8,9},{9,8},{10,11... | collective-permute-start | bytes 1572872 | tf_op jit(solution)/shard_map/ppermute | solution.py:138
  440.2 16.4 %collective-permute-start.38 = (bf16[512,512]{1,0:T(8,128)(2,1)}, bf16[512,512]{1,0:T(8,128)(2,1)}, u32[]{:S(2)}, u32[]{:S(2)}) collective-permute-start(bf16[512,512]{1,0:T(8,128)(2,1)} %get-tuple-element.80), channel_id=1, source_target_pairs={{0,1},{1,0},{2,3},{3,2},{4,5},{5,4},{6,7},{7,6},{8,9},{9,8},{10,11... | collective-permute-start | bytes 1572872 | tf_op jit(solution)/shard_map/ppermute | solution.py:138
  445.7 25.7 %collective-permute-start.42 = (bf16[512,512]{1,0:T(8,128)(2,1)S(1)}, bf16[512,512]{1,0:T(8,128)(2,1)}, u32[]{:S(2)}, u32[]{:S(2)}) collective-permute-start(bf16[512,512]{1,0:T(8,128)(2,1)S(1)} %add_convert_fusion.1), channel_id=1, source_target_pairs={{0,4},{1,5},{2,6},{3,7},{4,0},{5,1},{6,2},{7,3},{8,12},{9,13},{10,... | collective-permute-start | bytes 1572872 | tf_op jit(solution)/shard_map/ppermute | solution.py:138
  445.9 32.8 %collective-permute-start.43 = (bf16[512,512]{1,0:T(8,128)(2,1)S(1)}, bf16[512,512]{1,0:T(8,128)(2,1)}, u32[]{:S(2)}, u32[]{:S(2)}) collective-permute-start(bf16[512,512]{1,0:T(8,128)(2,1)S(1)} %add_convert_fusion.2), channel_id=1, source_target_pairs={{0,6},{1,7},{2,4},{3,5},{4,2},{5,3},{6,0},{7,1},{8,14},{9,15},{10,... | collective-permute-start | bytes 1572872 | tf_op jit(solution)/shard_map/ppermute | solution.py:138
  450.2 21.2 %collective-permute-start.44 = (bf16[512,512]{1,0:T(8,128)(2,1)S(1)}, bf16[512,512]{1,0:T(8,128)(2,1)}, u32[]{:S(2)}, u32[]{:S(2)}) collective-permute-start(bf16[512,512]{1,0:T(8,128)(2,1)S(1)} %add_convert_fusion), channel_id=1, source_target_pairs={{0,2},{1,3},{2,0},{3,1},{4,6},{5,7},{6,4},{7,5},{8,10},{9,11},{10,... | collective-permute-start | bytes 1572872 | tf_op jit(solution)/shard_map/ppermute | solution.py:138
  452.1 1.2 collective-permute-start.45
  453.3 2.8 collective-permute-start.46
  (33 other events, 836.5 us)
